TPU v7x, 8 devices: a whole 2x2x1 slice. The times are simulated.
8 devices in a mesh: fsdp: 8 (over z, y, x, core).
Axes of the slice: x: 2, y: 2, z: 1, core: 2. Of those that a mesh axis runs over, the one named last changes fastest.
Arguments:
- features: bfloat16 [24, 64, 1536], P('fsdp')
- tokens: int32 [24, 64], P('fsdp')
- embedding: bfloat16 [151936, 1536], replicated
- lm_head: bfloat16 [151936, 1536], replicated
- w_fc: bfloat16 [3072, 1536], P('fsdp')
- b_fc: bfloat16 [1536], P('fsdp')
- w_q: bfloat16 [1536, 12, 128], P('fsdp')
- w_k: bfloat16 [1536, 2, 128], P('fsdp')
- w_v: bfloat16 [1536, 2, 128], P('fsdp')
- w_o: bfloat16 [1536, 1536], P('fsdp')
- g_norm: bfloat16 [1536], P('fsdp')
- w_gate: bfloat16 [1536, 8960], P('fsdp')
- w_up: bfloat16 [1536, 8960], P('fsdp')
- w_down: bfloat16 [8960, 1536], P('fsdp')
Outputs:
- output 1: float32 [], replicated
- output 2: float32 [3072, 1536], P('fsdp')
- output 3: float32 [1536], P('fsdp')
- output 4: float32 [1536, 12, 128], P('fsdp')
- output 5: float32 [1536, 2, 128], P('fsdp')
- output 6: float32 [1536, 2, 128], P('fsdp')
- output 7: float32 [1536, 1536], P('fsdp')
- output 8: float32 [1536], P('fsdp')
- output 9: float32 [1536, 8960], P('fsdp')
- output 10: float32 [1536, 8960], P('fsdp')
- output 11: float32 [8960, 1536], P('fsdp')
All inputs are finite; a program needn't handle non-finite values.
Results may differ from a plain program's by a relative error of at most 0.02.
Values are sent between devices in bfloat16 or wider.
A program may use at most 3.75 GiB of HBM per device.

v0:
```python
import math
import functools
import jax
import jax.numpy as jnp
from jax import lax
from jax.sharding import PartitionSpec as P

AXIS_NAME = "fsdp"
ROPE_BASE = 10000
NORM_EPS = 1e-5
CLS_WEIGHT = 0.1


def rope_tables(seq_len, head_dim):
    half_dim = head_dim // 2
    inv_freq = jnp.exp(jnp.arange(half_dim, dtype=jnp.float32) * (-2.0 * math.log(ROPE_BASE) / head_dim))
    angles = jnp.arange(seq_len, dtype=jnp.float32)[:, None] * inv_freq[None, :]
    return jnp.cos(angles), jnp.sin(angles)


def apply_rope(projected, cos_tab, sin_tab):
    half_dim = projected.shape[-1] // 2
    first_half = projected[..., :half_dim]
    second_half = projected[..., half_dim:]
    cos_rows = cos_tab[None, :, None, :]
    sin_rows = sin_tab[None, :, None, :]
    return jnp.concatenate([first_half * cos_rows - second_half * sin_rows, second_half * cos_rows + first_half * sin_rows], axis=-1)


def attention_core(q_proj, k_proj, v_heads, cos_tab, sin_tab):
    batch_size, seq_len, head_count, head_dim = q_proj.shape
    kv_count = k_proj.shape[2]
    queries = apply_rope(q_proj, cos_tab, sin_tab).astype(jnp.bfloat16).reshape(batch_size, seq_len, kv_count, head_count // kv_count, head_dim)
    keys_rot = apply_rope(k_proj, cos_tab, sin_tab).astype(jnp.bfloat16)
    scores = jnp.einsum("bqkgd,bskd->bkgqs", queries, keys_rot, preferred_element_type=jnp.float32) * (1.0 / math.sqrt(head_dim))
    causal = lax.broadcasted_iota(jnp.int32, (seq_len, seq_len), 0) >= lax.broadcasted_iota(jnp.int32, (seq_len, seq_len), 1)
    attn_probs = jax.nn.softmax(jnp.where(causal, scores, -1e30), axis=-1).astype(jnp.bfloat16)
    attn_mixed = jnp.einsum("bkgqs,bskd->bqkgd", attn_probs, v_heads, preferred_element_type=jnp.float32).astype(jnp.bfloat16)
    return attn_mixed.reshape(batch_size, seq_len, head_count * head_dim)


def solution(mesh):
    shard_count = mesh.shape[AXIS_NAME]
    split_spec = P(AXIS_NAME)
    whole_spec = P()

    def gather_full(weight_shard):
        return lax.all_gather(weight_shard, AXIS_NAME, axis=0, tiled=True)

    def scatter_grad(grad_full):
        return lax.psum_scatter(grad_full, AXIS_NAME, scatter_dimension=0, tiled=True)

    def local_step(features, tokens, embedding, lm_head, w_fc, b_fc, w_q, w_k, w_v, w_o, g_norm, w_gate, w_up, w_down):
        batch_size, seq_len, model_width = features.shape
        inv_count = 1.0 / (batch_size * shard_count * (seq_len - 1))
        fc_full = gather_full(w_fc)
        bias_full = gather_full(b_fc)
        emb_rows = embedding[tokens]
        hidden0 = (jnp.einsum("bsd,de->bse", features, fc_full[:model_width], preferred_element_type=jnp.float32)
                   + jnp.einsum("bsd,de->bse", emb_rows, fc_full[model_width:], preferred_element_type=jnp.float32)
                   + bias_full.astype(jnp.float32)).astype(jnp.bfloat16)
        q_full = gather_full(w_q)
        k_full = gather_full(w_k)
        v_full = gather_full(w_v)
        q_proj = jnp.einsum("bsd,dhe->bshe", hidden0, q_full, preferred_element_type=jnp.float32)
        k_proj = jnp.einsum("bsd,dhe->bshe", hidden0, k_full, preferred_element_type=jnp.float32)
        v_heads = jnp.einsum("bsd,dhe->bshe", hidden0, v_full, preferred_element_type=jnp.float32).astype(jnp.bfloat16)
        cos_tab, sin_tab = rope_tables(seq_len, q_full.shape[2])
        attn_fn = functools.partial(attention_core, cos_tab=cos_tab, sin_tab=sin_tab)
        attn_mixed, attn_vjp = jax.vjp(attn_fn, q_proj, k_proj, v_heads)
        o_full = gather_full(w_o)
        hidden1 = (hidden0.astype(jnp.float32) + jnp.einsum("bsh,hd->bsd", attn_mixed, o_full, preferred_element_type=jnp.float32)).astype(jnp.bfloat16)
        h1_f32 = hidden1.astype(jnp.float32)
        inv_rms = lax.rsqrt(jnp.mean(h1_f32 * h1_f32, axis=-1, keepdims=True) + NORM_EPS)
        gain_full = gather_full(g_norm).astype(jnp.float32)
        normed = (h1_f32 * inv_rms * gain_full).astype(jnp.bfloat16)
        gate_full = gather_full(w_gate)
        up_full = gather_full(w_up)
        gate_pre = jnp.einsum("bsd,df->bsf", normed, gate_full, preferred_element_type=jnp.float32)
        up_pre = jnp.einsum("bsd,df->bsf", normed, up_full, preferred_element_type=jnp.float32)
        gate_sig = jax.nn.sigmoid(gate_pre)
        gate_act = gate_pre * gate_sig
        mlp_act = (gate_act * up_pre).astype(jnp.bfloat16)
        down_full = gather_full(w_down)
        draft_out = (h1_f32 + jnp.einsum("bsf,fd->bsd", mlp_act, down_full, preferred_element_type=jnp.float32)).astype(jnp.bfloat16)
        predicted = draft_out[:, :-1]
        target = features[:, 1:]
        pred_error = predicted.astype(jnp.float32) - target.astype(jnp.float32)
        abs_error = jnp.abs(pred_error)
        reg_total = jnp.sum(jnp.where(abs_error < 1.0, 0.5 * pred_error * pred_error, abs_error - 0.5)) / model_width
        target_prob = jax.nn.softmax(jnp.einsum("bsd,vd->bsv", target, lm_head, preferred_element_type=jnp.float32), axis=-1)
        log_q = jax.nn.log_softmax(jnp.einsum("bsd,vd->bsv", predicted, lm_head, preferred_element_type=jnp.float32), axis=-1)
        local_loss = reg_total - CLS_WEIGHT * jnp.sum(target_prob * log_q)
        total_loss = lax.psum(local_loss, AXIS_NAME) * inv_count

        logit_grad = ((jnp.exp(log_q) - target_prob) * (CLS_WEIGHT * inv_count)).astype(jnp.bfloat16)
        d_pred = jnp.clip(pred_error, -1.0, 1.0) * (inv_count / model_width) + jnp.einsum("bsv,vd->bsd", logit_grad, lm_head, preferred_element_type=jnp.float32)
        d_out = jnp.pad(d_pred, ((0, 0), (0, 1), (0, 0)))
        d_out_bf = d_out.astype(jnp.bfloat16)
        down_back = gather_full(w_down)
        grad_down = jnp.einsum("bsf,bsd->fd", mlp_act, d_out_bf, preferred_element_type=jnp.float32)
        d_act = jnp.einsum("bsd,fd->bsf", d_out_bf, down_back, preferred_element_type=jnp.float32)
        d_gate = (d_act * up_pre * gate_sig * (1.0 + gate_pre * (1.0 - gate_sig))).astype(jnp.bfloat16)
        d_up = (d_act * gate_act).astype(jnp.bfloat16)
        gate_back = gather_full(w_gate)
        up_back = gather_full(w_up)
        grad_gate = jnp.einsum("bsd,bsf->df", normed, d_gate, preferred_element_type=jnp.float32)
        grad_up = jnp.einsum("bsd,bsf->df", normed, d_up, preferred_element_type=jnp.float32)
        d_normed = (jnp.einsum("bsf,df->bsd", d_gate, gate_back, preferred_element_type=jnp.float32)
                    + jnp.einsum("bsf,df->bsd", d_up, up_back, preferred_element_type=jnp.float32))
        gain_back = gather_full(g_norm).astype(jnp.float32)
        grad_gain = jnp.sum(d_normed * h1_f32 * inv_rms, axis=(0, 1))
        gained = d_normed * gain_back
        d_hidden1 = d_out + inv_rms * gained - h1_f32 * (inv_rms * inv_rms * inv_rms) * jnp.mean(gained * h1_f32, axis=-1, keepdims=True)
        d_h1_bf = d_hidden1.astype(jnp.bfloat16)
        o_back = gather_full(w_o)
        grad_o = jnp.einsum("bsh,bsd->hd", attn_mixed, d_h1_bf, preferred_element_type=jnp.float32)
        d_mixed = jnp.einsum("bsd,hd->bsh", d_h1_bf, o_back, preferred_element_type=jnp.float32).astype(jnp.bfloat16)
        d_qproj, d_kproj, d_vheads = attn_vjp(d_mixed)
        d_q_bf = d_qproj.astype(jnp.bfloat16)
        d_k_bf = d_kproj.astype(jnp.bfloat16)
        q_back = gather_full(w_q)
        k_back = gather_full(w_k)
        v_back = gather_full(w_v)
        grad_q = jnp.einsum("bsd,bshe->dhe", hidden0, d_q_bf, preferred_element_type=jnp.float32)
        grad_k = jnp.einsum("bsd,bshe->dhe", hidden0, d_k_bf, preferred_element_type=jnp.float32)
        grad_v = jnp.einsum("bsd,bshe->dhe", hidden0, d_vheads, preferred_element_type=jnp.float32)
        d_hidden0 = (d_hidden1
                     + jnp.einsum("bshe,dhe->bsd", d_q_bf, q_back, preferred_element_type=jnp.float32)
                     + jnp.einsum("bshe,dhe->bsd", d_k_bf, k_back, preferred_element_type=jnp.float32)
                     + jnp.einsum("bshe,dhe->bsd", d_vheads, v_back, preferred_element_type=jnp.float32))
        d_h0_bf = d_hidden0.astype(jnp.bfloat16)
        grad_bias = jnp.sum(d_hidden0, axis=(0, 1))
        grad_fc = jnp.concatenate([jnp.einsum("bsd,bse->de", features, d_h0_bf, preferred_element_type=jnp.float32),
                                   jnp.einsum("bsd,bse->de", emb_rows, d_h0_bf, preferred_element_type=jnp.float32)], axis=0)
        return (total_loss, scatter_grad(grad_fc), scatter_grad(grad_bias), scatter_grad(grad_q), scatter_grad(grad_k), scatter_grad(grad_v),
                scatter_grad(grad_o), scatter_grad(grad_gain), scatter_grad(grad_gate), scatter_grad(grad_up), scatter_grad(grad_down))

    return jax.shard_map(local_step, mesh=mesh, in_specs=(split_spec, split_spec, whole_spec, whole_spec) + (split_spec,) * 10,
                         out_specs=(whole_spec,) + (split_spec,) * 10, check_vma=False)
```

profile of v0, /device:TPU:0, one launch (start us, length us, event | category | flops | bytes accessed | tf_op | source)
XLA Modules:
  0.0 2345.3 jit_solution(15726472241413870771)
XLA Ops:
  7.2 0.7 all-gather.7.cloned.1.call-update
  8.0 0.7 all-gather.9.cloned.1.call-update
  8.7 0.7 all-gather.11.cloned.1.call-update
  12.5 22.2 all_gather.40
  35.3 23.2 all-reduce.10
  59.1 0.8 fusion.105
  59.9 16.5 all_gather.41
  77.0 6.2 gather_fusion
  83.2 225.4 %fusion.116 = (f32[3,63]{1,0:T(4,128)S(1)}, f32[3,63,151936]{2,1,0:T(8,128)}) fusion(bf16[151936,1536]{1,0:T(8,128)(2,1)} %param.17, bf16[3,64,1536]{2,1,0:T(8,128)(2,1)S(1)} %copy-done.20), kind=kOutput, calls=%fused_computation.161 | convolution fusion | flops 88243970048 | bytes 582201600 | tf_op jit(solution)/shard_map/bsd,vd->bsv/dot_general | solution.py:91
  308.6 40.5 %fusion.7 = f32[3,63]{1,0:T(4,128)} fusion(f32[3,63,151936]{2,1,0:T(8,128)} %get-tuple-element.76, f32[3,63]{1,0:T(4,128)S(1)} %get-tuple-element.75), kind=kLoop, calls=%fused_computation.12 | loop fusion | flops 57431620 | bytes 114865128 | tf_op jit(solution)/shard_map/reduce_sum | solution.py:91
  349.1 3.6 fusion.25
  352.7 1.5 copy-done.77
  354.2 1.1 fusion.65
  356.4 3.6 fusion.33
  360.7 0.8 fusion.84
  361.8 1.3 copy-done.10
  364.1 0.8 copy-done.18
  366.4 3.7 multiply_reduce_fusion.3
  371.6 15.0 fusion.22
  386.7 18.7 all-gather.15.cloned.1.call-done
  405.4 20.7 multiply_convert_fusion.4
  426.1 110.6 %all-gather.17.cloned.1.call-done = bf16[8960,1536]{1,0:T(8,128)(2,1)} async-done(((bf16[1120,1536]{1,0:T(8,128)(2,1)}), bf16[8960,1536]{1,0:T(8,128)(2,1)}) %all-gather.17.cloned.1.call-update) | async-done | bytes 27525136 | tf_op jit(solution)/shard_map/all_gather | solution.py:48
  536.7 12.7 fusion.14
  549.4 1.1 fusion.76
  550.4 218.8 %fusion.115 = (f32[3,63]{1,0:T(4,128)S(1)}, f32[3,63,151936]{2,1,0:T(8,128)}) fusion(bf16[3,63,1536]{2,1,0:T(8,128)(2,1)S(1)} %get-tuple-element.52, bf16[151936,1536]{1,0:T(8,128)(2,1)} %param.17), kind=kOutput, calls=%fused_computation.160 | convolution fusion | flops 88243970048 | bytes 582192384 | tf_op jit(solution)/shard_map/bsd,vd->bsv/dot_general | solution.py:92
  769.3 35.8 %exponential_reduce_fusion = f32[3,63]{1,0:T(4,128)S(1)} fusion(f32[3,63,151936]{2,1,0:T(8,128)} %get-tuple-element.74, f32[3,63]{1,0:T(4,128)S(1)} %get-tuple-element.73), kind=kLoop, calls=%fused_computation.9 | loop fusion | flops 57431620 | bytes 114865128 | tf_op jit(solution)/shard_map/jit(log_softmax)/reduce_sum | solution.py:92
  805.2 206.1 %fusion.37 = f32[3,63,1536]{2,1,0:T(8,128)S(1)} fusion(bf16[151936,1536]{1,0:T(8,128)(2,1)} %param.17, f32[3,63,151936]{2,1,0:T(8,128)} %get-tuple-element.74, f32[3,63]{1,0:T(4,128)S(1)} %log.9, f32[3,63]{1,0:T(4,128)S(1)} %get-tuple-element.73, f32[3,63]{1,0:T(4,128)S(1)} %copy-done.66, f32[3,63,151936]{2,1,0:T(8,128)} %get-tuple-element.76, ...), kind=kOutput, calls=%fused_computation.57 | convolution fusion | flops 88418009088 | bytes 698800064 | tf_op jit(solution)/shard_map/bsv,vd->bsd/dot_general | solution.py:97
  1011.2 20.1 multiply_convert_fusion.3
  1031.4 16.0 fusion.16
  1047.4 16.8 multiply_reduce_fusion.1
  1064.2 1.6 multiply_subtract_fusion
  1065.8 4.0 fusion.56
  1069.9 1.5 reshape.121
  1071.5 2.0 fusion.74
  1073.5 0.7 copy-done.59
  1074.2 0.9 fusion.80
  1076.2 1.6 convolution_bitcast_fusion.8
  1077.8 1.0 copy-done.19
  1078.8 1.5 fusion.83
  1080.9 1.6 convolution_bitcast_fusion.7
  1082.6 0.8 copy-done.38
  1083.5 1.8 fusion.66
  1086.1 5.0 convolution_bitcast_fusion.6
  1091.1 1.0 copy-done.34
  1092.1 5.0 convolution_bitcast_fusion.3
  1097.4 0.9 copy-done.9
  1098.7 4.2 fusion.46
  1102.9 1.0 fusion.117
  1104.0 1.5 convolution_bitcast_fusion.5
  1105.5 1.4 convolution_bitcast_fusion.4
  1106.9 7.2 pad_maximum_fusion
  1114.2 1.0 copy-done.7
  1115.2 23.8 %convolution_bitcast_fusion.1 = f32[1536,8960]{1,0:T(8,128)} fusion(bf16[3,64,1536]{2,1,0:T(8,128)(2,1)S(1)} %copy-done.7, bf16[3,64,8960]{2,1,0:T(8,128)(2,1)} %get-tuple-element.53), kind=kOutput, calls=%fused_computation.17 | convolution fusion | flops 5284823040 | bytes 59080704 | tf_op jit(solution)/shard_map/bsd,bsf->df/dot_general | solution.py:107
  1139.4 28.8 %convolution_bitcast_fusion = f32[1536,8960]{1,0:T(8,128)} fusion(bf16[3,64,1536]{2,1,0:T(8,128)(2,1)S(1)} %copy-done.7, bf16[3,64,8960]{2,1,0:T(8,128)(2,1)} %get-tuple-element.54), kind=kOutput, calls=%fused_computation.16 | convolution fusion | flops 5284823040 | bytes 59080704 | tf_op jit(solution)/shard_map/bsd,bsf->df/dot_general | solution.py:108
  1168.2 1.2 copy-done.24
  1169.4 24.4 %convolution_bitcast_fusion.2 = f32[8960,1536]{1,0:T(8,128)} fusion(bf16[3,64,8960]{2,1,0:T(8,128)(2,1)} %get-tuple-element.71, f32[3,63,1536]{2,1,0:T(8,128)S(1)} %copy-done.24), kind=kOutput, calls=%fused_computation.18 | convolution fusion | flops 5284823040 | bytes 59652096 | tf_op jit(solution)/shard_map/bsf,bsd->fd/dot_general | solution.py:101
  1194.5 78.8 %multiply_reduce_fusion = f32[]{:T(128)} fusion(f32[3,63,151936]{2,1,0:T(8,128)} %get-tuple-element.74, f32[3,63]{1,0:T(4,128)S(1)} %copy-done.71, f32[3,63]{1,0:T(4,128)S(1)} %copy-done.69, f32[3,63]{1,0:T(4,128)S(1)} %copy-done.67, f32[3,63,151936]{2,1,0:T(8,128)} %get-tuple-element.76, f32[3,63]{1,0:T(4,128)S(1)} %copy-done.65), kind=kLoop, calls=%fused_computation.8 | loop fusion | flops 172295424 | bytes 229730256 | tf_op jit(solution)/shard_map/reduce_sum | solution.py:93
  1274.0 23.1 all-reduce.9
  1299.1 1.8 copy.57
  1300.9 1.8 copy.58
  1302.7 106.1 %reduce-scatter.9.cloned.1.call-done = f32[384,1536]{1,0:T(8,128)} async-done(((f32[3072,1536]{1,0:T(8,128)}), f32[384,1536]{1,0:T(8,128)}) %reduce-scatter.9.cloned.1.call-update) | async-done | bytes 2359312 | tf_op jit(solution)/shard_map/reduce_scatter | solution.py:51
  1408.8 309.5 %reduce-scatter.19.cloned.1.call-done = f32[192,8960]{1,0:T(8,128)} async-done(((f32[1536,8960]{1,0:T(8,128)}), f32[192,8960]{1,0:T(8,128)}) %reduce-scatter.19.cloned.1.call-update) | async-done | bytes 6881296 | tf_op jit(solution)/shard_map/reduce_scatter | solution.py:51
  1718.3 309.7 %reduce-scatter.21.cloned.1.call-done = f32[192,8960]{1,0:T(8,128)} async-done(((f32[1536,8960]{1,0:T(8,128)}), f32[192,8960]{1,0:T(8,128)}) %reduce-scatter.21.cloned.1.call-update) | async-done | bytes 6881296 | tf_op jit(solution)/shard_map/reduce_scatter | solution.py:51
  2027.9 309.5 %reduce-scatter.23.cloned.1.call-done = f32[1120,1536]{1,0:T(8,128)} async-done(((f32[8960,1536]{1,0:T(8,128)}), f32[1120,1536]{1,0:T(8,128)}) %reduce-scatter.23.cloned.1.call-update) | async-done | bytes 6881296 | tf_op jit(solution)/shard_map/reduce_scatter | solution.py:51
  (221 shorter events, 16.0 us)
Async XLA Ops:
  7.2 341.9 %all-gather.7.cloned.1.call-start = ((), (), s32[]{:S(2)}) async-start(), calls=%async_computation.8 | async-start | bytes 10616832 | tf_op jit(solution)/shard_map/all_gather | solution.py:48
  7.9 348.4 %all-gather.9.cloned.1.call-start = ((), (), s32[]{:S(2)}) async-start(), calls=%async_computation.9 | async-start | bytes 5308416 | tf_op jit(solution)/shard_map/all_gather | solution.py:48
  8.7 357.8 %all-gather.11.cloned.1.call-start = ((), (), s32[]{:S(2)}) async-start(), calls=%async_computation.10 | async-start | bytes 5308416 | tf_op jit(solution)/shard_map/all_gather | solution.py:48
  9.4 362.2 %all-gather.13.cloned.1.call-start = ((), (), s32[]{:S(2)}) async-start(), calls=%async_computation.11 | async-start | bytes 30965760 | tf_op jit(solution)/shard_map/all_gather | solution.py:48
  10.0 395.4 %all-gather.15.cloned.1.call-start = ((), (), s32[]{:S(2)}) async-start(), calls=%async_computation.12 | async-start | bytes 30965760 | tf_op jit(solution)/shard_map/all_gather | solution.py:48
  10.6 1.9 copy-start.53
  10.6 24.1 %copy-start.76 = (s32[3,64]{1,0:T(4,128)S(1)}, s32[3,64]{1,0:T(4,128)}, u32[]{:S(2)}) copy-start(s32[3,64]{1,0:T(4,128)} %param.15) | copy-start | bytes 2308
  10.6 24.2 %copy-start.78 = (bf16[192]{0:T(256)(128)(2,1)S(1)}, bf16[192]{0:T(256)(128)(2,1)}, u32[]{:S(2)}) copy-start(bf16[192]{0:T(256)(128)(2,1)} %param.19) | copy-start | bytes 1156
  10.6 24.4 %copy-start.79 = (bf16[192]{0:T(256)(128)(2,1)S(1)}, bf16[192]{0:T(256)(128)(2,1)}, u32[]{:S(2)}) copy-start(bf16[192]{0:T(256)(128)(2,1)} %param.24) | copy-start | bytes 1156
  10.6 526.1 %all-gather.17.cloned.1.call-start = ((), (), s32[]{:S(2)}) async-start(), calls=%async_computation.13 | async-start | bytes 30965760 | tf_op jit(solution)/shard_map/all_gather | solution.py:48
  11.2 48.7 %copy-start.54 = (bf16[192,2,128]{2,1,0:T(2,128)(2,1)S(1)}, bf16[192,2,128]{2,1,0:T(2,128)(2,1)}, u32[]{:S(2)}) copy-start(bf16[192,2,128]{2,1,0:T(2,128)(2,1)} %param.21) | copy-start | bytes 294916
  11.2 1287.9 %reduce-scatter.13.cloned.1.call-start = ((), (), s32[]{:S(2)}) async-start(), calls=%async_computation.16 | async-start | bytes 1769472 | tf_op jit(solution)/shard_map/reduce_scatter | solution.py:51
  77.0 6.2 copy-start.20
  308.6 40.5 %copy-start.63 = (f32[3,63]{1,0:T(4,128)}, f32[3,63]{1,0:T(4,128)S(1)}, u32[]{:S(2)}) copy-start(f32[3,63]{1,0:T(4,128)S(1)} %get-tuple-element.75) | copy-start | bytes 2272
  308.6 40.5 %copy-start.12 = (bf16[192,1536]{1,0:T(8,128)(2,1)S(1)}, bf16[192,1536]{1,0:T(8,128)(2,1)}, u32[]{:S(2)}) copy-start(bf16[192,1536]{1,0:T(8,128)(2,1)} %gather_fusion) | copy-start | bytes 1769476
  349.1 3.6 copy-start.73
  349.1 5.1 copy-start.77
  355.3 11.1 copy-start.4
  356.3 4.2 copy-start.37
  356.3 4.2 copy-start.39
  361.5 1.9 copy-start
  361.5 1.9 copy-start.45
  361.5 1.6 copy-start.10
  363.1 7.7 copy-start.48
  366.4 3.8 copy-start.33
  366.4 5.0 copy-start.55
  370.2 179.2 %copy-start.2 = (f32[3,64,1536]{2,1,0:T(8,128)}, f32[3,64,1536]{2,1,0:T(8,128)S(1)}, u32[]{:S(2)}) copy-start(f32[3,64,1536]{2,1,0:T(8,128)S(1)} %get-tuple-element.70) | copy-start | bytes 3538948
  370.8 15.9 copy-start.61
  371.6 33.8 %copy-start.6 = (bf16[3,64,1536]{2,1,0:T(8,128)(2,1)}, bf16[3,64,1536]{2,1,0:T(8,128)(2,1)S(1)}, u32[]{:S(2)}) copy-start(bf16[3,64,1536]{2,1,0:T(8,128)(2,1)S(1)} %multiply_convert_fusion.7) | copy-start | bytes 1769476
  550.4 218.8 %copy-start.35 = (bf16[3,63,1536]{2,1,0:T(8,128)(2,1)}, bf16[3,63,1536]{2,1,0:T(8,128)(2,1)S(1)}, u32[]{:S(2)}) copy-start(bf16[3,63,1536]{2,1,0:T(8,128)(2,1)S(1)} %get-tuple-element.52) | copy-start | bytes 1741828
  769.2 35.9 %copy-start.68 = (f32[3,63]{1,0:T(4,128)}, f32[3,63]{1,0:T(4,128)S(1)}, u32[]{:S(2)}) copy-start(f32[3,63]{1,0:T(4,128)S(1)} %get-tuple-element.73) | copy-start | bytes 2272
  769.2 35.9 %copy-start.21 = (bf16[3,64,1536]{2,1,0:T(8,128)(2,1)S(1)}, bf16[3,64,1536]{2,1,0:T(8,128)(2,1)}, u32[]{:S(2)}) copy-start(bf16[3,64,1536]{2,1,0:T(8,128)(2,1)} %param.14) | copy-start | bytes 1769476
  769.2 35.9 %copy-start.36 = (bf16[3,63,1536]{2,1,0:T(8,128)(2,1)S(1)}, bf16[3,63,1536]{2,1,0:T(8,128)(2,1)}, u32[]{:S(2)}) copy-start(bf16[3,63,1536]{2,1,0:T(8,128)(2,1)} %copy-done.35) | copy-start | bytes 1741828
  769.2 35.9 %copy-start.64 = (f32[3,63]{1,0:T(4,128)S(1)}, f32[3,63]{1,0:T(4,128)}, u32[]{:S(2)}) copy-start(f32[3,63]{1,0:T(4,128)} %copy-done.63) | copy-start | bytes 2272
  769.3 35.9 %copy-start.66 = (f32[3,63]{1,0:T(4,128)S(1)}, f32[3,63]{1,0:T(4,128)}, u32[]{:S(2)}) copy-start(f32[3,63]{1,0:T(4,128)} %fusion.7) | copy-start | bytes 2272
  805.1 206.1 %copy-start.70 = (f32[3,63]{1,0:T(4,128)}, f32[3,63]{1,0:T(4,128)S(1)}, u32[]{:S(2)}) copy-start(f32[3,63]{1,0:T(4,128)S(1)} %log.9) | copy-start | bytes 2272
  1011.2 52.9 %copy-start.23 = (f32[3,63,1536]{2,1,0:T(8,128)}, f32[3,63,1536]{2,1,0:T(8,128)S(1)}, u32[]{:S(2)}) copy-start(f32[3,63,1536]{2,1,0:T(8,128)S(1)} %fusion.37) | copy-start | bytes 3483652
  1031.4 16.0 copy-start.3
  1031.4 16.0 copy-start.56
  1031.4 16.0 copy-start.62
  1047.4 16.8 copy-start.72
  1069.8 1.6 copy-start.1
  1069.8 1.6 copy-start.42
  1069.8 1.6 copy-start.46
  1069.8 1.6 copy-start.52
  1069.9 1.6 copy-start.58
  1071.4 2.7 copy-start.15
  1071.4 2.7 copy-start.17
  1071.5 2.7 copy-start.49
  1071.5 2.7 copy-start.75
  1073.4 1.6 copy-start.80
  1077.8 223.1 %reduce-scatter.15.cloned.1.call-start = ((), (), s32[]{:S(2)}) async-start(), calls=%async_computation.17 | async-start | bytes 1769472 | tf_op jit(solution)/shard_map/reduce_scatter | solution.py:51
  1082.6 2.7 copy-start.29
  1082.6 2.7 copy-start.32
  1082.6 220.1 %reduce-scatter.11.cloned.1.call-start = ((), (), s32[]{:S(2)}) async-start(), calls=%async_computation.15 | async-start | bytes 10616832 | tf_op jit(solution)/shard_map/reduce_scatter | solution.py:51
  1091.1 211.6 %reduce-scatter.17.cloned.1.call-start = ((), (), s32[]{:S(2)}) async-start(), calls=%async_computation.18 | async-start | bytes 10616832 | tf_op jit(solution)/shard_map/reduce_scatter | solution.py:51
  1097.2 311.6 %reduce-scatter.9.cloned.1.call-start = ((), (), s32[]{:S(2)}) async-start(), calls=%async_computation.14 | async-start | bytes 21233664 | tf_op jit(solution)/shard_map/reduce_scatter | solution.py:51
  1098.7 4.2 copy-start.11
  1098.7 4.2 copy-start.44
  1114.2 604.1 %reduce-scatter.19.cloned.1.call-start = ((), (), s32[]{:S(2)}) async-start(), calls=%async_computation.19 | async-start | bytes 61931520 | tf_op jit(solution)/shard_map/reduce_scatter | solution.py:51
  1139.1 888.9 %reduce-scatter.21.cloned.1.call-start = ((), (), s32[]{:S(2)}) async-start(), calls=%async_computation.20 | async-start | bytes 61931520 | tf_op jit(solution)/shard_map/reduce_scatter | solution.py:51
  1168.2 1169.3 %reduce-scatter.23.cloned.1.call-start = ((), (), s32[]{:S(2)}) async-start(), calls=%async_computation.21 | async-start | bytes 61931520 | tf_op jit(solution)/shard_map/reduce_scatter | solution.py:51
  1194.5 79.5 %copy-start.57 = (f32[1536]{0:T(1024)S(1)}, f32[1536]{0:T(1024)}, u32[]{:S(2)}) copy-start(f32[1536]{0:T(1024)} %get-tuple-element.80) | copy-start | bytes 18436
  1194.5 79.5 %copy-start.74 = (f32[1536]{0:T(1024)S(1)}, f32[1536]{0:T(1024)}, u32[]{:S(2)}) copy-start(f32[1536]{0:T(1024)} %get-tuple-element.44) | copy-start | bytes 18436
  (31 other events, 28.6 us)
Sparse Core Ops, SparseCore 0:
  9.8 62.5 all-gather.6
  74.2 33.4 all-gather.8
  109.5 33.2 all-gather.10
  144.4 129.6 all-gather.12
  275.7 129.6 all-gather.14
  407.0 129.5 all-gather.16
  1077.9 29.9 reduce-scatter.12
  1111.1 30.0 reduce-scatter.14
  1145.2 68.2 reduce-scatter.10
  1217.4 69.0 reduce-scatter.16
  1290.6 118.1 reduce-scatter.8
  1412.7 305.4 reduce-scatter.18
  1722.4 305.4 reduce-scatter.20
  2031.9 305.4 reduce-scatter.22
where the time goes:
time: 2350 us
  waiting for transfers between devices  1170 us (50%)
  matrix products  874 us (37%)
  other arithmetic  172 us (7%)
  blocking collectives  85 us (4%)
  local copies, waits for them, and re-layouts  27.3 us (1%)
    reduce_scatter x8, waiting for transfers between devices, scatter_grad(): lax.psum_scatter(grad_full, AXIS_NAME, scatter_dimension=0, tiled=True)  1030 us
    dot_general x1, matrix products, local_step(): jnp.einsum('bsd,vd->bsv', target, lm_head, preferred_element_type=jnp.flo...  225 us
    dot_general x1, matrix products, local_step(): jnp.einsum('bsd,vd->bsv', predicted, lm_head, preferred_element_type=jnp....  219 us
    dot_general x1, matrix products, local_step(): jnp.einsum('bsv,vd->bsd', logit_grad, lm_head, preferred_element_type=jnp...  206 us
    all_gather x6, waiting for transfers between devices, gather_full(): return lax.all_gather(weight_shard, AXIS_NAME, axis=0, tiled=True)  129 us
    reduce_sum x1, other arithmetic, local_step(): local_loss = reg_total - CLS_WEIGHT * jnp.sum(target_prob * log_q)  78.8 us
  transfers between devices with their start and end apart: 14, of which 6 were waited for; matrix products, arithmetic and copies ran while one was open for 22% of the time, Pallas kernels for 0%

commit v1 on v0

v1 whole, which is shorter than its diff:
```python
import math
import functools
import jax
import jax.numpy as jnp
from jax import lax
from jax.experimental import pallas as pl
from jax.experimental.pallas import tpu as pltpu
from jax.sharding import PartitionSpec as P

AXIS_NAME = "fsdp"
ROPE_BASE = 10000
NORM_EPS = 1e-5
CLS_WEIGHT = 0.1
F32 = jnp.float32
BF16 = jnp.bfloat16

SUB = 768
PER = 3
TILE = SUB * PER
COLS = 256
VMEM = 60 * 1024 * 1024
NEG = -1e30


def dot(a, b, ca, cb):
    return lax.dot_general(a, b, (((ca,), (cb,)), ((), ())), preferred_element_type=F32)


def rope_tables(seq_len, head_dim):
    half_dim = head_dim // 2
    inv_freq = jnp.exp(jnp.arange(half_dim, dtype=F32) * (-2.0 * math.log(ROPE_BASE) / head_dim))
    angles = jnp.arange(seq_len, dtype=F32)[:, None] * inv_freq[None, :]
    return jnp.cos(angles), jnp.sin(angles)


def apply_rope(projected, cos_tab, sin_tab):
    half_dim = projected.shape[-1] // 2
    first_half = projected[..., :half_dim]
    second_half = projected[..., half_dim:]
    cos_rows = cos_tab[None, :, None, :]
    sin_rows = sin_tab[None, :, None, :]
    return jnp.concatenate([first_half * cos_rows - second_half * sin_rows, second_half * cos_rows + first_half * sin_rows], axis=-1)


def attention_core(q_proj, k_proj, v_heads, cos_tab, sin_tab):
    batch_size, seq_len, head_count, head_dim = q_proj.shape
    kv_count = k_proj.shape[2]
    queries = apply_rope(q_proj, cos_tab, sin_tab).astype(BF16).reshape(batch_size, seq_len, kv_count, head_count // kv_count, head_dim)
    keys_rot = apply_rope(k_proj, cos_tab, sin_tab).astype(BF16)
    scores = jnp.einsum("bqkgd,bskd->bkgqs", queries, keys_rot, preferred_element_type=F32) * (1.0 / math.sqrt(head_dim))
    causal = lax.broadcasted_iota(jnp.int32, (seq_len, seq_len), 0) >= lax.broadcasted_iota(jnp.int32, (seq_len, seq_len), 1)
    attn_probs = jax.nn.softmax(jnp.where(causal, scores, -1e30), axis=-1).astype(BF16)
    attn_mixed = jnp.einsum("bkgqs,bskd->bqkgd", attn_probs, v_heads, preferred_element_type=F32).astype(BF16)
    return attn_mixed.reshape(batch_size, seq_len, head_count * head_dim)


def logits_kernel(info_ref, x_ref, h_ref, z_ref, m_ref, l_ref):
    step = pl.program_id(0)

    @pl.when(step == 0)
    def _():
        m_ref[...] = jnp.full(m_ref.shape, NEG, F32)
        l_ref[...] = jnp.zeros(l_ref.shape, F32)

    skip = jnp.where(step == 0, info_ref[1], 0)
    lane = lax.broadcasted_iota(jnp.int32, (1, 128), 1)

    def stats(c):
        parts = [z_ref[:, c * COLS + k * 128:c * COLS + (k + 1) * 128] for k in range(COLS // 128)]
        m_old = m_ref[...]
        m_new = m_old
        for part in parts:
            m_new = jnp.maximum(m_new, part)
        total = l_ref[...] * jnp.exp(m_old - m_new)
        for part in parts:
            total = total + jnp.exp(part - m_new)
        m_ref[...] = m_new
        l_ref[...] = total

    count = TILE // COLS
    for c in range(count):
        z = dot(x_ref[...], h_ref[c * COLS:(c + 1) * COLS, :], 1, 1)
        if c == 0:
            z_ref[:, :128] = jnp.where(lane < skip, NEG, z[:, :128])
            z_ref[:, 128:COLS] = z[:, 128:]
        else:
            z_ref[:, c * COLS:(c + 1) * COLS] = z
        if c > 0:
            stats(c - 1)
    stats(count - 1)


def logits_pass(info, x, lm_head, steps):
    rows, width = x.shape
    return pl.pallas_call(
        logits_kernel,
        grid_spec=pltpu.PrefetchScalarGridSpec(
            num_scalar_prefetch=1,
            grid=(steps,),
            in_specs=[pl.BlockSpec((rows, width), lambda i, s: (0, 0)),
                      pl.BlockSpec((pl.Element(TILE), pl.Element(width)), lambda i, s: (pl.multiple_of(s[0] + i * TILE, 16), 0))],
            out_specs=[pl.BlockSpec((rows, TILE), lambda i, s: (0, i)),
                       pl.BlockSpec((rows, 128), lambda i, s: (0, 0)),
                       pl.BlockSpec((rows, 128), lambda i, s: (0, 0))]),
        out_shape=[jax.ShapeDtypeStruct((rows, steps * TILE), F32),
                   jax.ShapeDtypeStruct((rows, 128), F32),
                   jax.ShapeDtypeStruct((rows, 128), F32)],
        compiler_params=pltpu.CompilerParams(dimension_semantics=("arbitrary",), vmem_limit_bytes=VMEM),
        cost_estimate=pl.CostEstimate(flops=2 * rows * width * steps * TILE, bytes_accessed=steps * TILE * (2 * width + 4 * rows),
                                      transcendentals=2 * rows * steps * TILE),
        name="vocab_logits",
    )(info, x, lm_head)


def grad_kernel(steps, info_ref, zt_ref, zq_ref, ha_ref, hb_ref, hc_ref, lt_ref, lq_ref, scale_ref, dy_ref, cross_ref, ga, gb, gc):
    step = pl.program_id(0)

    def fill(g_ref, index):
        part_cross = jnp.zeros(cross_ref.shape, F32)
        for k in range(SUB // 128):
            cols = slice(index * SUB + k * 128, index * SUB + (k + 1) * 128)
            log_q = zq_ref[:, cols] - lq_ref[...]
            prob = jnp.exp(zt_ref[:, cols] - lt_ref[...])
            part_cross = part_cross + prob * log_q
            g_ref[:, k * 128:(k + 1) * 128] = ((jnp.exp(log_q) - prob) * scale_ref[...]).astype(BF16)
        cross_ref[...] += part_cross

    @pl.when(step == 0)
    def _():
        dy_ref[...] = jnp.zeros(dy_ref.shape, F32)
        cross_ref[...] = jnp.zeros(cross_ref.shape, F32)
        gc[...] = jnp.zeros(gc.shape, BF16)

    @pl.when(step < steps)
    def _():
        dy_ref[...] += dot(gc[...], ha_ref[...], 1, 0)
        fill(ga, 0)
        dy_ref[...] += dot(ga[...], hb_ref[...], 1, 0)
        fill(gb, 1)
        dy_ref[...] += dot(gb[...], hc_ref[...], 1, 0)
        fill(gc, 2)

    @pl.when(step == steps)
    def _():
        dy_ref[...] += dot(gc[...], ha_ref[...], 1, 0)


def grad_pass(info, zt, zq, lm_head, lse_t, lse_q, scale, steps):
    rows = zt.shape[0]
    width = lm_head.shape[1]
    last = steps * PER - 1

    def head_spec(shift):
        return pl.BlockSpec((pl.Element(SUB), pl.Element(width)),
                            lambda i, s: (pl.multiple_of(s[0] + jnp.clip(i * PER + shift, 0, last) * SUB, 16), 0))

    z_spec = pl.BlockSpec((rows, TILE), lambda i, s: (0, jnp.minimum(i, steps - 1)))
    row_spec = pl.BlockSpec((rows, 128), lambda i, s: (0, 0))
    return pl.pallas_call(
        functools.partial(grad_kernel, steps),
        grid_spec=pltpu.PrefetchScalarGridSpec(
            num_scalar_prefetch=1,
            grid=(steps + 1,),
            in_specs=[z_spec, z_spec, head_spec(-1), head_spec(0), head_spec(1), row_spec, row_spec, row_spec],
            out_specs=[pl.BlockSpec((rows, width), lambda i, s: (0, 0)), row_spec],
            scratch_shapes=[pltpu.VMEM((rows, SUB), BF16)] * PER),
        out_shape=[jax.ShapeDtypeStruct((rows, width), F32), jax.ShapeDtypeStruct((rows, 128), F32)],
        compiler_params=pltpu.CompilerParams(dimension_semantics=("arbitrary",), vmem_limit_bytes=VMEM),
        cost_estimate=pl.CostEstimate(flops=2 * rows * width * steps * TILE, bytes_accessed=steps * TILE * (2 * width + 8 * rows),
                                      transcendentals=2 * rows * steps * TILE),
        name="vocab_grad",
    )(info, zt, zq, lm_head, lm_head, lm_head, lse_t, lse_q, scale)


def lane_lse(m, l):
    top = jnp.max(m, axis=1, keepdims=True)
    return top, jnp.sum(l * jnp.exp(m - top), axis=1, keepdims=True)


def solution(mesh):
    n = mesh.shape[AXIS_NAME]
    split_spec = P(AXIS_NAME)
    whole_spec = P()
    pair = [(i, i ^ 1) for i in range(n)]

    def gather(x):
        return lax.all_gather(x, AXIS_NAME, axis=0, tiled=True)

    def swap(x):
        return lax.ppermute(x, AXIS_NAME, pair)

    def spread(x):
        return lax.all_to_all(x, AXIS_NAME, 0, 0, tiled=True)

    def by_owner(x):
        return x.reshape(x.shape[0], n, x.shape[1] // n).transpose(1, 0, 2)

    def local_step(features, tokens, embedding, lm_head, w_fc, b_fc, w_q, w_k, w_v, w_o, g_norm, w_gate, w_up, w_down):
        batch, seq, width = features.shape
        rows = batch * seq
        vocab = lm_head.shape[0]
        heads, head_dim = w_q.shape[1:]
        kvs = w_k.shape[1]
        qw, kw = heads * head_dim, kvs * head_dim
        shard = w_q.shape[0]
        hidden = w_gate.shape[1]
        inv_count = 1.0 / (batch * n * (seq - 1))
        me = lax.axis_index(AXIS_NAME)
        core = lax.rem(me, 2)

        per_group = hidden // 128 // (n // 4)
        wide = -(-per_group // 4) * 128
        starts = [128 * per_group * (j // 4) + wide * (j % 4) for j in range(n)]
        ends = [starts[j + 1] if j + 1 < n else hidden for j in range(n)]
        spare = starts[-1] + wide - hidden
        place = lax.rem(me, 4)
        shift = wide - hidden // n

        steps = -(-(vocab // 2) // TILE)
        span = steps * TILE
        info = jnp.stack([jnp.where(core == 0, 0, vocab - span), jnp.where(core == 0, 0, 2 * span - vocab)]).astype(jnp.int32)

        f_rows = features.reshape(rows, width)

        def next_rows(x):
            x = x.reshape(batch, seq, width)
            return jnp.concatenate([x[:, 1:], x[:, -1:]], axis=1).reshape(rows, width)

        target = jnp.concatenate([next_rows(f_rows), next_rows(swap(f_rows))], axis=0)
        fc_full = gather(w_fc)
        small = jnp.pad(jnp.stack([b_fc, g_norm], axis=1), ((0, 0), (0, 126)))
        packed = gather(jnp.concatenate([w_q.reshape(shard, qw), w_k.reshape(shard, kw), w_v.reshape(shard, kw), small, w_o], axis=1))
        qkv_full = packed[:, :qw + 2 * kw]
        bias = packed[:, qw + 2 * kw].astype(F32)
        gain = packed[:, qw + 2 * kw + 1].astype(F32)
        o_full = packed[:, qw + 2 * kw + 128:]

        def tiles(w):
            w = jnp.pad(w, ((0, 0), (0, spare)))
            return jnp.stack([w[:, s:s + wide] for s in starts])

        gu = spread(jnp.concatenate([tiles(w_gate), tiles(w_up)], axis=2)).reshape(width, 2 * wide)
        up_rows = lax.ppermute(w_down[:128], AXIS_NAME, [(j + 1, j) for j in range(n - 1) if j % 4 != 3])
        down = lax.dynamic_slice(jnp.concatenate([w_down, up_rows], axis=0), (shift * place, 0), (wide, width))

        zt, m_t, l_t = logits_pass(info, target, lm_head, steps)
        fc_full, zt, m_t, l_t = lax.optimization_barrier((fc_full, zt, m_t, l_t))

        emb_rows = embedding[tokens].reshape(rows, width)
        hidden0 = (dot(f_rows, fc_full[:width], 1, 0) + dot(emb_rows, fc_full[width:], 1, 0) + bias).astype(BF16)
        qkv = dot(hidden0, qkv_full, 1, 0)
        q_proj = qkv[:, :qw].reshape(batch, seq, heads, head_dim)
        k_proj = qkv[:, qw:qw + kw].reshape(batch, seq, kvs, head_dim)
        v_heads = qkv[:, qw + kw:].astype(BF16).reshape(batch, seq, kvs, head_dim)
        cos_tab, sin_tab = rope_tables(seq, head_dim)
        attn_fn = functools.partial(attention_core, cos_tab=cos_tab, sin_tab=sin_tab)
        mixed, attn_vjp = jax.vjp(attn_fn, q_proj, k_proj, v_heads)
        mixed_rows = mixed.reshape(rows, qw)
        hidden1 = (hidden0.astype(F32) + dot(mixed_rows, o_full, 1, 0)).astype(BF16)
        h1 = hidden1.astype(F32)
        inv_rms = lax.rsqrt(jnp.mean(h1 * h1, axis=-1, keepdims=True) + NORM_EPS)
        normed = (h1 * inv_rms * gain).astype(BF16)

        normed_all = gather(normed)
        pre = dot(normed_all, gu, 1, 0)
        gate_pre, up_pre = pre[:, :wide], pre[:, wide:]
        gate_sig = jax.nn.sigmoid(gate_pre)
        gate_act = gate_pre * gate_sig
        act = (gate_act * up_pre).astype(BF16)
        mlp_out = lax.psum_scatter(dot(act, down, 1, 0), AXIS_NAME, scatter_dimension=0, tiled=True)
        draft_out = (h1 + mlp_out).astype(BF16)

        draft_pair = jnp.concatenate([draft_out, swap(draft_out)], axis=0)
        zq, m_q, l_q = logits_pass(info, draft_pair, lm_head, steps)
        inputs_all = spread(jnp.concatenate([by_owner(jnp.concatenate([f_rows, emb_rows], axis=1)), by_owner(hidden0), by_owner(mixed_rows)], axis=2))
        inputs_all = inputs_all.reshape(n * rows, 4 * shard)
        top_t, sum_t = lane_lse(m_t, l_t)
        top_q, sum_q = lane_lse(m_q, l_q)
        mine = jnp.concatenate([top_t, sum_t, top_q, sum_q], axis=1)
        theirs = swap(mine)
        theirs = jnp.concatenate([theirs[rows:], theirs[:rows]], axis=0)

        def merged(k):
            top = jnp.maximum(mine[:, k], theirs[:, k])
            total = mine[:, k + 1] * jnp.exp(mine[:, k] - top) + theirs[:, k + 1] * jnp.exp(theirs[:, k] - top)
            return top + jnp.log(total)

        valid = (lax.rem(lax.broadcasted_iota(jnp.int32, (2 * rows, 1), 0), seq) < seq - 1).astype(F32)

        def lanes(x):
            return jnp.broadcast_to(x.reshape(2 * rows, 1), (2 * rows, 128))

        dy, cross = grad_pass(info, zt, zq, lm_head, lanes(merged(0)), lanes(merged(2)), lanes(valid * (CLS_WEIGHT * inv_count)), steps)
        dy, inputs_all = lax.optimization_barrier((dy, inputs_all))
        dy_own = dy[:rows] + swap(dy[rows:])

        error = (draft_out.astype(F32) - next_rows(f_rows).astype(F32)) * valid[:rows]
        abs_error = jnp.abs(error)
        reg_total = jnp.sum(jnp.where(abs_error < 1.0, 0.5 * error * error, abs_error - 0.5)) / width
        local_loss = reg_total - CLS_WEIGHT * jnp.sum(cross * valid)

        d_out = (jnp.clip(error, -1.0, 1.0) * (inv_count / width) + dy_own) * valid[:rows]
        d_out_all = gather(d_out.astype(BF16))
        d_act = dot(d_out_all, down, 1, 1)
        d_gate = (d_act * up_pre * gate_sig * (1.0 + gate_pre * (1.0 - gate_sig))).astype(BF16)
        d_up = (d_act * gate_act).astype(BF16)
        d_gu = jnp.concatenate([d_gate, d_up], axis=1)
        d_normed = lax.psum_scatter(dot(d_gu, gu, 1, 1), AXIS_NAME, scatter_dimension=0, tiled=True)
        grad_gu = dot(normed_all, d_gu, 0, 0).reshape(n, shard, 2 * wide)
        d_normed, grad_gu = lax.optimization_barrier((d_normed, grad_gu))
        grad_gu = spread(grad_gu)
        grad_gate = jnp.concatenate([grad_gu[j][:, :ends[j] - starts[j]] for j in range(n)], axis=1)
        grad_up = jnp.concatenate([grad_gu[j][:, wide:wide + ends[j] - starts[j]] for j in range(n)], axis=1)
        grad_down = dot(act, d_out_all, 0, 0)
        edge = 3 * shift
        from_prev = lax.ppermute(grad_down[wide - edge:], AXIS_NAME, [(j, j + 1) for j in range(n - 1) if j % 4 != 3])
        grad_down = lax.dynamic_slice(jnp.concatenate([from_prev, grad_down], axis=0), (edge - shift * place, 0), (hidden // n, width))

        gained = d_normed * gain
        d_hidden1 = d_out + inv_rms * gained - h1 * (inv_rms * inv_rms * inv_rms) * jnp.mean(gained * h1, axis=-1, keepdims=True)
        d_h1 = d_hidden1.astype(BF16)
        sums = lax.psum(jnp.concatenate([jnp.sum(d_normed * h1 * inv_rms, axis=0), jnp.full((128,), local_loss, F32)]), AXIS_NAME)
        total_loss = sums[width] * inv_count
        grad_gain = lax.dynamic_slice(sums, (me * shard,), (shard,))
        d_h1_all = gather(d_h1)
        d_mixed = dot(d_h1, o_full, 1, 1).astype(BF16)
        d_q, d_k, d_v = attn_vjp(d_mixed.reshape(mixed.shape))
        d_qkv = jnp.concatenate([d_q.reshape(rows, qw).astype(BF16), d_k.reshape(rows, kw).astype(BF16), d_v.reshape(rows, kw)], axis=1)
        d_h0 = (d_hidden1 + dot(d_qkv, qkv_full, 1, 1)).astype(BF16)
        d_qkv_all = gather(d_qkv)
        d_h0_all = gather(d_h0)
        grad_o = dot(inputs_all[:, 3 * shard:], d_h1_all, 0, 0)
        grad_qkv = dot(inputs_all[:, 2 * shard:3 * shard], d_qkv_all, 0, 0)
        grad_fc = dot(inputs_all[:, :2 * shard], d_h0_all, 0, 0)
        grad_bias = jnp.sum(lax.dynamic_slice(d_h0_all, (0, me * shard), (n * rows, shard)).astype(F32), axis=0)
        return (total_loss, grad_fc, grad_bias, grad_qkv[:, :qw].reshape(w_q.shape), grad_qkv[:, qw:qw + kw].reshape(w_k.shape),
                grad_qkv[:, qw + kw:].reshape(w_v.shape), grad_o, grad_gain, grad_gate, grad_up, grad_down)

    return jax.shard_map(local_step, mesh=mesh, in_specs=(split_spec, split_spec, whole_spec, whole_spec) + (split_spec,) * 10,
                         out_specs=(whole_spec,) + (split_spec,) * 10, check_vma=False)
```

time: 2350 us -> 1180 us (0.50)
  waiting for transfers between devices: 1170 us -> 246 us
  matrix products: 874 us -> 127 us
  Pallas kernels: 0 us -> 416 us
  blocking collectives: 85 us -> 214 us
  other arithmetic: 172 us -> 45.1 us
  local copies, waits for them, and re-layouts: 27.3 us -> 83.7 us
    reduce_scatter x8 -> x2, waiting for transfers between devices: 1030 us -> 117 us  [the longest x1 68 us: local_step(): lax.psum_scatter(dot(act, down, 1, 0), AXIS_NAME, scatter_dimension=0, ti...]
    dot_general x28 -> x15, matrix products: 867 us -> 121 us  [dot(): lax.dot_general(a, b, (((ca,), (cb,)), ((), ())), preferred_element_type=...]
    pallas_call x0 -> x3, Pallas kernels: none -> 416 us  [the longest x2 261 us: logits_pass(): pl.pallas_call(logits_kernel, grid_spec=pltpu.PrefetchScalarGridSpec(num_...]
    psum x1, blocking collectives: 23.1 us -> 214 us  [local_step(): lax.psum(jnp.concatenate([jnp.sum(d_normed * h1 * inv_rms, axis=0), jnp.f...]
    reduce_sum x5 -> x7, other arithmetic: 156 us -> 8.79 us  [the longest x1 2.48 us: local_step(): jnp.sum(jnp.where(abs_error < 1.0, 0.5 * error * error, abs_error - 0.5))]
    all_gather x6 -> x7, waiting for transfers between devices: 129 us -> 34.5 us  [gather(): return lax.all_gather(x, AXIS_NAME, axis=0, tiled=True)]
    all_to_all x0 -> x3, waiting for transfers between devices: none -> 90.1 us  [spread(): return lax.all_to_all(x, AXIS_NAME, 0, 0, tiled=True)]
    all_gather x2 -> x0, blocking collectives: 38.7 us -> none  [gather_full(): return lax.all_gather(weight_shard, AXIS_NAME, axis=0, tiled=True)]
  transfers between devices with their start and end apart: 14 -> 18, of which waited for: 6 -> 5; matrix products, arithmetic and copies ran while one was open for 22% -> 10% of each run, Pallas kernels for 0% -> 25%
where the time goes in v1:
time: 1180 us; the launch traced here: 1170 us
  Pallas kernels  416 us (35%)
  waiting for transfers between devices  246 us (21%)
  blocking collectives  214 us (18%)
  matrix products  127 us (11%)
  local copies, waits for them, and re-layouts  83.7 us (7%)
  other arithmetic  45.1 us (4%)
  between operations  18.6 us (2%)
  starting transfers between devices  18.5 us (2%)
    pallas_call x2, Pallas kernels, logits_pass(): pl.pallas_call(logits_kernel, grid_spec=pltpu.PrefetchScalarGridSpec(num_...  261 us
    psum x1, blocking collectives, local_step(): lax.psum(jnp.concatenate([jnp.sum(d_normed * h1 * inv_rms, axis=0), jnp.f...  214 us
    pallas_call x1, Pallas kernels, grad_pass(): pl.pallas_call(functools.partial(grad_kernel, steps), grid_spec=pltpu.Pre...  155 us
    dot_general x15, matrix products, dot(): lax.dot_general(a, b, (((ca,), (cb,)), ((), ())), preferred_element_type=...  121 us
    all_to_all x3, waiting for transfers between devices, spread(): return lax.all_to_all(x, AXIS_NAME, 0, 0, tiled=True)  90.1 us
    reduce_scatter x1, waiting for transfers between devices, local_step(): lax.psum_scatter(dot(act, down, 1, 0), AXIS_NAME, scatter_dimension=0, ti...  68 us
    reduce_scatter x1, waiting for transfers between devices, local_step(): lax.psum_scatter(dot(d_gu, gu, 1, 1), AXIS_NAME, scatter_dimension=0, til...  48.7 us
    unnamed x186, local copies, waits for them, and re-layouts  42.9 us
  transfers between devices with their start and end apart: 18, of which 5 were waited for; matrix products, arithmetic and copies ran while one was open for 10% of the time, Pallas kernels for 25%

profile of v1, /device:TPU:0, one launch (start us, length us, event | category | flops | bytes accessed | tf_op | source)
XLA Modules:
  0.0 1169.2 jit_solution(11079916681536516911)
XLA Ops:
  14.9 5.1 gather_fusion
  20.2 1.7 bitcast_dynamic-update-slice_fusion.8
  21.9 1.7 bitcast_dynamic-update-slice_fusion.7
  26.7 1.8 copy-done.24
  29.8 131.5 %vocab_logits.2 = (f32[384,76032]{1,0:T(8,128)}, f32[384,128]{1,0:T(8,128)}, f32[384,128]{1,0:T(8,128)}) custom-call(s32[2]{0:T(128)} %pad_add_fusion.info_ref, bf16[384,1536]{1,0:T(8,128)(2,1)} %pad_maximum_fusion.5.x_ref, bf16[151936,1536]{1,0:T(8,128)(2,1)} %hc_ref.1), custom_call_target="tpu_custom_call" | custom-call | flops 89690996736 | bytes 350355456 | tf_op jit(solution)/shard_map/vocab_logits/pallas_call | solution.py:95
  161.3 4.4 fusion.29
  165.8 1.6 convert_reduce_fusion.1
  167.4 3.8 fusion.38
  172.0 4.2 fusion.4
  183.1 3.5 fusion.58
  188.4 1.8 bitcast_dynamic-update-slice_fusion.11
  190.2 1.8 bitcast_dynamic-update-slice_fusion.10
  192.0 1.8 bitcast_dynamic-update-slice_fusion.9
  193.8 2.1 fusion.81
  195.9 6.9 pad_maximum_fusion
  202.8 5.1 all-to-all-start
  208.9 1.5 collective-permute-start.1
  210.4 90.1 %all-to-all-done = bf16[8,192,2304]{2,1,0:T(8,128)(2,1)} async-done(((bf16[8,192,2304]{2,1,0:T(8,128)(2,1)}), bf16[8,192,2304]{2,1,0:T(8,128)(2,1)}, u32[]{:S(2)}, u32[]{:S(2)}) %all-to-all-start) | async-done | bytes 7077920 | tf_op jit(solution)/shard_map/all_to_all | solution.py:193
  300.6 15.0 %fusion.121 = f32[1536,2304]{1,0:T(8,128)S(1)} fusion(bf16[1536,1536]{1,0:T(8,128)(2,1)} %all-gather.12.cloned.1.call-done, bf16[1536,2304]{1,0:T(8,128)(2,1)} %bitcast.30), kind=kOutput, calls=%fused_computation.233 | convolution fusion | flops 10871635968 | bytes 25952256 | tf_op jit(solution)/shard_map/dot_general | solution.py:26
  315.6 2.2 multiply_convert_fusion.2
  317.8 3.8 copy-done.3
  321.5 1.8 copy-done.25
  323.3 9.4 fusion.109
  332.8 68.0 %reduce-scatter.3.cloned.1.call-done = f32[192,1536]{1,0:T(8,128)} async-done(((f32[1536,1536]{1,0:T(8,128)}), f32[192,1536]{1,0:T(8,128)}) %reduce-scatter.3.cloned.1.call-update) | async-done | bytes 1179664 | tf_op jit(solution)/shard_map/reduce_scatter | solution.py:270
  400.8 2.5 fusion.57
  403.3 1.8 concatenate.84
  405.3 1.6 maximum_bitcast_fusion
  408.1 2.4 reshape.242
  410.5 2.2 pad_maximum_fusion.6.x_ref
  412.6 129.5 %vocab_logits.3 = (f32[384,76032]{1,0:T(8,128)}, f32[384,128]{1,0:T(8,128)}, f32[384,128]{1,0:T(8,128)}) custom-call(s32[2]{0:T(128)} %pad_add_fusion.info_ref, bf16[384,1536]{1,0:T(8,128)(2,1)} %pad_maximum_fusion.6.x_ref, bf16[151936,1536]{1,0:T(8,128)(2,1)} %hc_ref.1), custom_call_target="tpu_custom_call" | custom-call | flops 89690996736 | bytes 350355456 | tf_op jit(solution)/shard_map/vocab_logits/pallas_call | solution.py:95
  545.6 1.9 copy.98
  547.5 3.1 all-to-all-start.1
  553.2 155.0 %vocab_grad.1 = (f32[384,1536]{1,0:T(8,128)}, f32[384,128]{1,0:T(8,128)}) custom-call(s32[2]{0:T(128)} %pad_add_fusion.info_ref, f32[384,76032]{1,0:T(8,128)} %get-tuple-element.31.zt_ref, f32[384,76032]{1,0:T(8,128)} %get-tuple-element.32.zq_ref, bf16[151936,1536]{1,0:T(8,128)(2,1)} %hc_ref.1, bf16[151936,1536]{1,0:T(8,128)(2,1)} %hc_ref.1, ...), custom_call_target="tpu_custom_call" | custom-call | flops 89690996736 | bytes 467140608 | tf_op jit(solution)/shard_map/vocab_grad/pallas_call | solution.py:159
  708.2 1.3 slice.306
  710.1 2.5 collective-permute-done.4
  712.6 2.5 fusion.116
  715.2 34.5 %all-gather.14.cloned.1.call-done = bf16[1536,1536]{1,0:T(8,128)(2,1)} async-done(((bf16[192,1536]{1,0:T(8,128)(2,1)}), bf16[1536,1536]{1,0:T(8,128)(2,1)}) %all-gather.14.cloned.1.call-update) | async-done | bytes 4718608 | tf_op jit(solution)/shard_map/all_gather | solution.py:187
  749.7 13.5 %multiply_convert_fusion.1 = (bf16[1536,1152]{1,0:T(8,128)(2,1)S(1)}, bf16[1536,1152]{1,0:T(8,128)(2,1)S(1)}) fusion(f32[1536,2304]{1,0:T(8,128)} %copy-done.3, bf16[1536,1536]{1,0:T(8,128)(2,1)} %all-gather.14.cloned.1.call-done, s32[]{:T(128)S(6)} %select_n.42, bf16[1120,1536]{1,0:T(8,128)(2,1)} %param.27, bf16[128,1536]{1,0:T(8,128)(2,1)S(1)} %copy-done.76), kind=kOutput, calls=%fused_computation.6 | convolution fusion | flops 5465899008 | bytes 29786116 | tf_op jit(solution)/shard_map/dot_general | solution.py:26
  763.2 1.8 copy-done.77
  766.2 15.1 %fusion.11 = f32[1536,1536]{1,0:T(8,128)} fusion(bf16[1536,2304]{1,0:T(8,128)(2,1)} %bitcast.30, bf16[1536,1152]{1,0:T(8,128)(2,1)S(1)} %get-tuple-element.100, bf16[1536,1152]{1,0:T(8,128)(2,1)S(1)} %get-tuple-element.99), kind=kOutput, calls=%fused_computation.20 | convolution fusion | flops 10885791744 | bytes 23592960 | tf_op jit(solution)/shard_map/dot_general | solution.py:26
  782.6 18.5 %fusion.10 = f32[1536,2304]{1,0:T(8,128)} fusion(bf16[1536,1536]{1,0:T(8,128)(2,1)} %all-gather.12.cloned.1.call-done, bf16[1536,1152]{1,0:T(8,128)(2,1)} %copy-done.78, bf16[1536,1152]{1,0:T(8,128)(2,1)} %copy-done.77), kind=kOutput, calls=%fused_computation.19 | convolution fusion | flops 10885791744 | bytes 25952256 | tf_op jit(solution)/shard_map/dot_general | solution.py:26
  801.1 48.7 %reduce-scatter.5.cloned.1.call-done = f32[192,1536]{1,0:T(8,128)} async-done(((f32[1536,1536]{1,0:T(8,128)}), f32[192,1536]{1,0:T(8,128)}) %reduce-scatter.5.cloned.1.call-update) | async-done | bytes 1179664 | tf_op jit(solution)/shard_map/reduce_scatter | solution.py:308
  849.9 1.6 fusion.66
  851.5 2.7 fusion.113
  854.2 5.1 fusion.32
  859.2 2.7 reshape_reshape.3
  862.0 1.5 fusion.73
  863.5 1.9 fusion.55
  868.1 1.5 fusion.44
  870.9 5.8 fusion.35
  877.5 4.2 all-to-all-start.2
  882.5 8.8 fusion.122
  891.3 2.9 copy-done.13
  894.2 2.3 collective-permute-start.5
  898.5 6.7 fusion.1
  905.2 214.0 %psum.7 = f32[1664]{0:T(1024)S(1)} all-reduce(f32[1664]{0:T(1024)S(1)} %concatenate.88), channel_id=1, replica_groups=mesh['fsdp'=8] {'fsdp'}, use_global_device_ids=true, to_apply=%region_12.13 | all-reduce | flops 1664 | bytes 13312 | tf_op jit(solution)/shard_map/psum | solution.py:322
  1121.0 2.2 convert_reduce_fusion
  1123.2 4.9 fusion.75
  1128.2 4.7 fusion.67
  1132.9 4.5 fusion.77
  1140.1 9.8 slice_bitcast_fusion
  1149.9 1.7 slice_dynamic-update-slice_fusion.5
  1156.2 2.9 copy-done.65
  1159.0 2.3 copy-done.66
  (289 shorter events, 47.2 us)
Async XLA Ops:
  7.2 6.5 copy-start.28
  7.2 7.5 copy-start.74
  7.2 154.1 %all-gather.8.cloned.1.call-start = ((), (), s32[]{:S(2)}) async-start(), calls=%async_computation.5 | async-start | bytes 10616832 | tf_op jit(solution)/shard_map/all_gather | solution.py:187
  8.0 157.8 %all-gather.10.cloned.1.call-start = ((), (), s32[]{:S(2)}) async-start(), calls=%async_computation.6 | async-start | bytes 12828672 | tf_op jit(solution)/shard_map/all_gather | solution.py:187
  13.6 286.9 %all-gather.12.cloned.1.call-start = ((), (), s32[]{:S(2)}) async-start(), calls=%async_computation.7 | async-start | bytes 5308416 | tf_op jit(solution)/shard_map/all_gather | solution.py:187
  13.7 13.0 %collective-permute-start = (bf16[192,1536]{1,0:T(8,128)(2,1)S(1)}, bf16[192,1536]{1,0:T(8,128)(2,1)S(1)}, u32[]{:S(2)}, u32[]{:S(2)}) collective-permute-start(bf16[192,1536]{1,0:T(8,128)(2,1)S(1)} %bitcast.193), channel_id=1, source_target_pairs={{0,1},{1,0},{2,3},{3,2},{4,5},{5,4},{6,7},{7,6}} | collective-permute-start | bytes 1769480 | tf_op jit(solution)/shard_map/ppermute | solution.py:190
  19.9 147.5 %copy-start.31 = (bf16[192,1536]{1,0:T(8,128)(2,1)}, bf16[192,1536]{1,0:T(8,128)(2,1)S(1)}, u32[]{:S(2)}) copy-start(bf16[192,1536]{1,0:T(8,128)(2,1)S(1)} %gather_fusion) | copy-start | bytes 1769476
  19.9 4.7 copy-start.5
  20.0 159.9 %copy-start.63 = (pred[64,64]{0,1:T(8,128)(4,1)}, pred[64,64]{0,1:T(8,128)(4,1)S(1)}, u32[]{:S(2)}) copy-start(pred[64,64]{0,1:T(8,128)(4,1)S(1)} %iota_compare_fusion.1) | copy-start | bytes 12292
  20.1 158.4 %copy-start.40 = (f32[64,64]{1,0:T(8,128)}, f32[64,64]{1,0:T(8,128)S(1)}, u32[]{:S(2)}) copy-start(f32[64,64]{1,0:T(8,128)S(1)} %get-tuple-element.143) | copy-start | bytes 49156
  20.1 158.4 %copy-start.42 = (f32[64,64]{1,0:T(8,128)}, f32[64,64]{1,0:T(8,128)S(1)}, u32[]{:S(2)}) copy-start(f32[64,64]{1,0:T(8,128)S(1)} %get-tuple-element.144) | copy-start | bytes 49156
  20.2 4.7 copy-start.4
  20.2 8.5 copy-start.10
  167.4 19.9 %copy-start.61 = (f32[1536]{0:T(1024)}, f32[1536]{0:T(1024)S(1)}, u32[]{:S(2)}) copy-start(f32[1536]{0:T(1024)S(1)} %get-tuple-element.87) | copy-start | bytes 18436
  179.5 3.6 copy-start.54
  179.6 3.6 copy-start.48
  180.5 6.2 copy-start.56
  186.7 214.1 %copy-start.8 = (bf16[192,1536]{1,0:T(8,128)(2,1)}, bf16[192,1536]{1,0:T(8,128)(2,1)S(1)}, u32[]{:S(2)}) copy-start(bf16[192,1536]{1,0:T(8,128)(2,1)S(1)} %get-tuple-element.148) | copy-start | bytes 1769476
  187.3 8.6 copy-start.68
  202.8 97.8 %all-to-all-start = ((bf16[8,192,2304]{2,1,0:T(8,128)(2,1)}), bf16[8,192,2304]{2,1,0:T(8,128)(2,1)}, u32[]{:S(2)}, u32[]{:S(2)}) async-start(bf16[8,192,2304]{2,1,0:T(8,128)(2,1)} %pad_maximum_fusion), calls=%async_computation | async-start | bytes 14155776 | tf_op jit(solution)/shard_map/all_to_all | solution.py:193
  207.8 193.0 %reduce-scatter.3.cloned.1.call-start = ((), (), s32[]{:S(2)}) async-start(), calls=%async_computation.8 | async-start | bytes 10616832 | tf_op jit(solution)/shard_map/reduce_scatter | solution.py:270
  208.9 112.6 %collective-permute-start.1 = (bf16[128,1536]{1,0:T(8,128)(2,1)S(1)}, bf16[128,1536]{1,0:T(8,128)(2,1)S(1)}, u32[]{:S(2)}, u32[]{:S(2)}) collective-permute-start(bf16[128,1536]{1,0:T(8,128)(2,1)S(1)} %slice.297), channel_id=1, source_target_pairs={{1,0},{2,1},{3,2},{5,4},{6,5},{7,6}} | collective-permute-start | bytes 1179656 | tf_op jit(solution)/shard_map/ppermute | solution.py:243
  315.6 5.9 copy-start.3
  315.6 7.7 copy-start.67
  323.3 9.4 copy-start.75
  332.8 68.0 %copy-start.11 = (bf16[3,64,1536]{2,1,0:T(8,128)(2,1)S(1)}, bf16[3,64,1536]{2,1,0:T(8,128)(2,1)}, u32[]{:S(2)}) copy-start(bf16[3,64,1536]{2,1,0:T(8,128)(2,1)} %copy-done.10) | copy-start | bytes 1769476
  332.8 72.3 %copy-start.29 = (bf16[3,64,1536]{2,1,0:T(8,128)(2,1)S(1)}, bf16[3,64,1536]{2,1,0:T(8,128)(2,1)}, u32[]{:S(2)}) copy-start(bf16[3,64,1536]{2,1,0:T(8,128)(2,1)} %param.14) | copy-start | bytes 1769476
  332.8 72.3 %copy-start.71 = (f32[192,1]{0,1:T(1,128)}, f32[192,1]{0,1:T(1,128)S(1)}, u32[]{:S(2)}) copy-start(f32[192,1]{0,1:T(1,128)S(1)} %compare_convert_fusion) | copy-start | bytes 2308
  400.8 6.1 copy-start.44
  400.8 6.2 copy-start.60
  403.3 7.2 copy-start.20
  403.3 7.2 collective-permute-start.2
  412.6 132.4 %copy-start.22 = (bf16[8,192,384]{2,0,1:T(8,128)(2,1)S(1)}, bf16[8,192,384]{2,0,1:T(8,128)(2,1)}, u32[]{:S(2)}) copy-start(bf16[8,192,384]{2,0,1:T(8,128)(2,1)} %maximum_bitcast_fusion) | copy-start | bytes 3538948
  412.6 132.4 %copy-start.26 = (bf16[192,8,192]{2,1,0:T(8,128)(2,1)S(1)}, bf16[192,8,192]{2,1,0:T(8,128)(2,1)}, u32[]{:S(2)}) copy-start(bf16[192,8,192]{2,1,0:T(8,128)(2,1)} %reshape.242) | copy-start | bytes 1769476
  544.5 6.1 collective-permute-start.3
  547.5 160.7 %all-to-all-start.1 = ((bf16[8,192,768]{2,1,0:T(8,128)(2,1)}), bf16[8,192,768]{2,1,0:T(8,128)(2,1)}, u32[]{:S(2)}, u32[]{:S(2)}) async-start(bf16[8,192,768]{2,1,0:T(8,128)(2,1)} %copy.98), calls=%async_computation.2 | async-start | bytes 4718592 | tf_op jit(solution)/shard_map/all_to_all | solution.py:193
  550.6 199.1 %all-gather.14.cloned.1.call-start = ((), (), s32[]{:S(2)}) async-start(), calls=%async_computation.9 | async-start | bytes 5308416 | tf_op jit(solution)/shard_map/all_gather | solution.py:187
  553.2 159.4 %copy-start.12 = (bf16[3,64,1536]{2,1,0:T(8,128)(2,1)S(1)}, bf16[3,64,1536]{2,1,0:T(8,128)(2,1)}, u32[]{:S(2)}) copy-start(bf16[3,64,1536]{2,1,0:T(8,128)(2,1)} %copy-done.10) | copy-start | bytes 1769476
  553.2 159.4 %copy-start.21 = (bf16[192,1536]{1,0:T(8,128)(2,1)S(1)}, bf16[192,1536]{1,0:T(8,128)(2,1)}, u32[]{:S(2)}) copy-start(bf16[192,1536]{1,0:T(8,128)(2,1)} %copy-done.20) | copy-start | bytes 1769476
  553.2 159.4 %copy-start.72 = (f32[192,1]{0,1:T(1,128)S(1)}, f32[192,1]{0,1:T(1,128)}, u32[]{:S(2)}) copy-start(f32[192,1]{0,1:T(1,128)} %copy-done.71) | copy-start | bytes 2308
  709.5 40.1 %copy-start.76 = (bf16[128,1536]{1,0:T(8,128)(2,1)S(1)}, bf16[128,1536]{1,0:T(8,128)(2,1)}, u32[]{:S(2)}) copy-start(bf16[128,1536]{1,0:T(8,128)(2,1)} %copy-done.75) | copy-start | bytes 1179652
  709.5 3.0 collective-permute-start.4
  715.1 134.7 %reduce-scatter.5.cloned.1.call-start = ((), (), s32[]{:S(2)}) async-start(), calls=%async_computation.10 | async-start | bytes 10616832 | tf_op jit(solution)/shard_map/reduce_scatter | solution.py:308
  781.3 339.7 %all-gather.16.cloned.1.call-start = ((), (), s32[]{:S(2)}) async-start(), calls=%async_computation.11 | async-start | bytes 5308416 | tf_op jit(solution)/shard_map/all_gather | solution.py:187
  782.6 67.3 %copy-start.9 = (bf16[192,1536]{1,0:T(8,128)(2,1)S(1)}, bf16[192,1536]{1,0:T(8,128)(2,1)}, u32[]{:S(2)}) copy-start(bf16[192,1536]{1,0:T(8,128)(2,1)} %copy-done.8) | copy-start | bytes 1769476
  782.6 67.3 %copy-start.62 = (f32[1536]{0:T(1024)S(1)}, f32[1536]{0:T(1024)}, u32[]{:S(2)}) copy-start(f32[1536]{0:T(1024)} %copy-done.61) | copy-start | bytes 18436
  782.6 67.3 %copy-start.69 = (f32[192]{0:T(256)S(1)}, f32[192]{0:T(256)}, u32[]{:S(2)}) copy-start(f32[192]{0:T(256)} %copy-done.68) | copy-start | bytes 2308
  782.6 68.9 %copy-start.73 = (f32[192]{0:T(256)S(1)}, f32[192]{0:T(256)}, u32[]{:S(2)}) copy-start(f32[192]{0:T(256)} %get-tuple-element.141) | copy-start | bytes 2308
  854.2 5.1 copy-start.32
  854.2 7.9 copy-start.34
  854.2 9.3 copy-start.7
  854.2 9.3 copy-start.64
  859.2 6.2 copy-start.36
  859.2 6.2 copy-start.38
  862.0 3.5 copy-start.55
  870.3 6.4 copy-start.30
  876.7 246.5 %all-gather.20.cloned.1.call-start = ((), (), s32[]{:S(2)}) async-start(), calls=%async_computation.13 | async-start | bytes 5308416 | tf_op jit(solution)/shard_map/all_gather | solution.py:187
  877.5 262.6 %all-to-all-start.2 = ((f32[8,192,2304]{2,1,0:T(8,128)}), f32[8,192,2304]{2,1,0:T(8,128)}, u32[]{:S(2)}, u32[]{:S(2)}) async-start(f32[8,192,2304]{2,1,0:T(8,128)} %bitcast.187), calls=%async_computation.4 | async-start | bytes 28311552 | tf_op jit(solution)/shard_map/all_to_all | solution.py:193
  881.7 251.2 %all-gather.18.cloned.1.call-start = ((), (), s32[]{:S(2)}) async-start(), calls=%async_computation.12 | async-start | bytes 7077888 | tf_op jit(solution)/shard_map/all_gather | solution.py:187
  882.4 14.7 %copy-start.59 = (f32[384,128]{1,0:T(8,128)S(1)}, f32[384,128]{1,0:T(8,128)}, u32[]{:S(2)}) copy-start(f32[384,128]{1,0:T(8,128)} %get-tuple-element.40) | copy-start | bytes 589828
  894.2 4.3 collective-permute-start.5
  1123.2 4.9 copy-start.2
  1154.6 6.7 copy-start.1
  1156.2 5.2 copy-start.66
  (33 other events, 58.5 us)
Sparse Core Ops, SparseCore 0:
  9.8 55.9 all-gather.7
  68.2 61.4 all-gather.9
  188.5 49.6 all-gather.11
  332.9 67.8 reduce-scatter.2
  715.2 34.3 all-gather.13
  781.4 68.4 reduce-scatter.4
  876.9 117.5 all-gather.15
  996.9 65.7 all-gather.19
  1065.0 44.6 all-gather.17

commit v2 on v1

--- a/solution.py
+++ b/solution.py
@@ -54,7 +54,7 @@
     return attn_mixed.reshape(batch_size, seq_len, head_count * head_dim)
 
 
-def logits_kernel(info_ref, x_ref, h_ref, z_ref, m_ref, l_ref):
+def logits_kernel(info_ref, x_ref, ha_ref, hb_ref, hc_ref, z_ref, m_ref, l_ref):
     step = pl.program_id(0)
 
     @pl.when(step == 0)
@@ -79,7 +79,8 @@
 
     count = TILE // COLS
     for c in range(count):
-        z = dot(x_ref[...], h_ref[c * COLS:(c + 1) * COLS, :], 1, 1)
+        h_ref, part = (ha_ref, hb_ref, hc_ref)[c * COLS // SUB], c % (SUB // COLS)
+        z = dot(x_ref[...], h_ref[part * COLS:(part + 1) * COLS, :], 1, 1)
         if c == 0:
             z_ref[:, :128] = jnp.where(lane < skip, NEG, z[:, :128])
             z_ref[:, 128:COLS] = z[:, 128:]
@@ -97,8 +98,9 @@
         grid_spec=pltpu.PrefetchScalarGridSpec(
             num_scalar_prefetch=1,
             grid=(steps,),
-            in_specs=[pl.BlockSpec((rows, width), lambda i, s: (0, 0)),
-                      pl.BlockSpec((pl.Element(TILE), pl.Element(width)), lambda i, s: (pl.multiple_of(s[0] + i * TILE, 16), 0))],
+            in_specs=[pl.BlockSpec((rows, width), lambda i, s: (0, 0))] + [
+                pl.BlockSpec((pl.Element(SUB), pl.Element(width)), lambda i, s, k=k: (pl.multiple_of(s[0] + i * TILE + k * SUB, 16), 0))
+                for k in range(PER)],
             out_specs=[pl.BlockSpec((rows, TILE), lambda i, s: (0, i)),
                        pl.BlockSpec((rows, 128), lambda i, s: (0, 0)),
                        pl.BlockSpec((rows, 128), lambda i, s: (0, 0))]),
@@ -109,7 +111,7 @@
         cost_estimate=pl.CostEstimate(flops=2 * rows * width * steps * TILE, bytes_accessed=steps * TILE * (2 * width + 4 * rows),
                                       transcendentals=2 * rows * steps * TILE),
         name="vocab_logits",
-    )(info, x, lm_head)
+    )(info, x, lm_head, lm_head, lm_head)
 
 
 def grad_kernel(steps, info_ref, zt_ref, zq_ref, ha_ref, hb_ref, hc_ref, lt_ref, lq_ref, scale_ref, dy_ref, cross_ref, ga, gb, gc):
@@ -172,6 +174,209 @@
     )(info, zt, zq, lm_head, lm_head, lm_head, lse_t, lse_q, scale)
 
 
+def exchange_kernel(compute, n_inputs, n_outputs, reduced, *refs):
+    own, inputs = refs[0], refs[1:n_inputs]
+    blocks, out = refs[n_inputs], refs[n_inputs + 1]
+    outputs = refs[n_inputs + 2:n_inputs + n_outputs]
+    part, pair_in, relay_x, relay_y, from_x, from_y, gsend, grecv, dsend, drecv, ssend, srecv = refs[n_inputs + n_outputs:n_inputs + n_outputs + 12]
+    rows = own.shape[0]
+    half = rows // 2
+    me = lax.axis_index(AXIS_NAME)
+    core, x, y = me % 2, (me // 2) % 2, me // 4
+    mate = me + 1 - 2 * core
+    xn = me + 2 - 4 * x
+    yn = me + 4 - 8 * y
+
+    def remote(src, dst, send, recv, to):
+        return pltpu.make_async_remote_copy(src_ref=src, dst_ref=dst, send_sem=send, recv_sem=recv, device_id=(to,),
+                                            device_id_type=pl.DeviceIdType.MESH)
+
+    def slot(s, first=0, count=rows):
+        return blocks.at[pl.ds(s * rows + first, count)]
+
+    to_mate = remote(own, slot(1), gsend.at[0], grecv.at[0], mate)
+    to_x = remote(own, slot(2), gsend.at[1], grecv.at[1], xn)
+    to_y = remote(own, slot(4), gsend.at[2], grecv.at[2], yn)
+    x_to_y = remote(slot(2, 0, half), slot(6, 0, half), gsend.at[3], grecv.at[3], yn)
+    y_to_x = remote(slot(4, half, half), slot(6, half, half), gsend.at[4], grecv.at[4], xn)
+    x_to_mate = remote(slot(2), slot(3), gsend.at[5], grecv.at[5], mate)
+    y_to_mate = remote(slot(4), slot(5), gsend.at[6], grecv.at[6], mate)
+    d_to_mate = remote(slot(6), slot(7), gsend.at[7], grecv.at[7], mate)
+    pair = [remote(part.at[2 * k + 1], pair_in.at[k], dsend.at[k], drecv.at[k], mate) for k in range(4)]
+    top, bottom = pl.ds(0, half), pl.ds(half, half)
+    diag_x = remote(part.at[6, top], relay_x, ssend.at[0], srecv.at[0], xn)
+    diag_y = remote(part.at[6, bottom], relay_y, ssend.at[1], srecv.at[1], yn)
+    x_top = remote(part.at[2, top], from_x.at[top], ssend.at[2], srecv.at[2], xn)
+    x_bottom = remote(part.at[2, bottom], from_x.at[bottom], ssend.at[3], srecv.at[3], xn)
+    y_top = remote(part.at[4, top], from_y.at[top], ssend.at[4], srecv.at[4], yn)
+    y_bottom = remote(part.at[4, bottom], from_y.at[bottom], ssend.at[5], srecv.at[5], yn)
+
+    barrier = pltpu.get_barrier_semaphore()
+    for other in (mate, xn, yn):
+        pl.semaphore_signal(barrier, inc=1, device_id=(other,), device_id_type=pl.DeviceIdType.MESH)
+    blocks[pl.ds(0, rows)] = own[...]
+    pl.semaphore_wait(barrier, 3)
+    to_x.start()
+    to_y.start()
+    to_mate.start()
+
+    def body(s, carry):
+        @pl.when(s == 1)
+        def _():
+            to_mate.wait_recv()
+
+        @pl.when(s == 2)
+        def _():
+            to_x.wait_recv()
+            x_to_y.start()
+            x_to_mate.start()
+            to_y.wait_recv()
+            y_to_x.start()
+            y_to_mate.start()
+
+        @pl.when(s == 3)
+        def _():
+            x_to_mate.wait_recv()
+
+        @pl.when(s == 5)
+        def _():
+            y_to_mate.wait_recv()
+
+        @pl.when(s == 6)
+        def _():
+            x_to_y.wait_recv()
+            y_to_x.wait_recv()
+            d_to_mate.start()
+
+        @pl.when(s == 7)
+        def _():
+            d_to_mate.wait_recv()
+
+        compute(s, blocks, part, inputs, outputs)
+
+        @pl.when(s == 1)
+        def _():
+            pair[0].start()
+
+        @pl.when(s == 3)
+        def _():
+            pair[1].start()
+
+        @pl.when(s == 4)
+        def _():
+            pair[1].wait_recv()
+            part[2] += pair_in[1]
+            x_top.start()
+
+        @pl.when(s == 5)
+        def _():
+            pair[2].start()
+
+        @pl.when(s == 6)
+        def _():
+            pair[2].wait_recv()
+            part[4] += pair_in[2]
+            y_bottom.start()
+
+        return carry
+
+    lax.fori_loop(0, 8, body, 0)
+    pair[3].start()
+    pair[3].wait_recv()
+    part[6] += pair_in[3]
+    diag_x.start()
+    diag_y.start()
+    pair[0].wait_recv()
+    part[0] += pair_in[0]
+    diag_y.wait_recv()
+    part[2, bottom] += relay_y[...]
+    x_bottom.start()
+    diag_x.wait_recv()
+    part[4, top] += relay_x[...]
+    y_top.start()
+    x_top.wait_recv()
+    y_bottom.wait_recv()
+    x_bottom.wait_recv()
+    y_top.wait_recv()
+    out[...] = part[0] + from_x[...] + from_y[...]
+    small = []
+    if reduced:
+        scaled, scalar = inputs[-2:]
+        sums = outputs[-1]
+        mine, theirs, rsend, rrecv = refs[n_inputs + n_outputs + 12:]
+        mine[0, :, :scaled.shape[1]] = jnp.broadcast_to(jnp.sum(out[...] * scaled[...], axis=0, keepdims=True), (8, scaled.shape[1]))
+        mine[0, :, scaled.shape[1]:] = scalar[...]
+        for k, other in enumerate((mate, xn, yn)):
+            copy = remote(mine.at[k], theirs.at[k], rsend.at[k], rrecv.at[k], other)
+            copy.start()
+            copy.wait_recv()
+            small.append(copy)
+            if k < 2:
+                mine[k + 1] = mine[k] + theirs[k]
+            else:
+                sums[...] = mine[k] + theirs[k]
+    for copy in small + [to_mate, to_x, to_y, x_to_y, y_to_x, x_to_mate, y_to_mate, d_to_mate] + pair + [diag_x, diag_y, x_top, x_bottom, y_top, y_bottom]:
+        copy.wait_send()
+
+
+CHUNK = 384
+
+
+def forward_block(s, blocks, part, inputs, outputs):
+    gu, down = inputs
+    act, = outputs
+    wide = down.shape[0]
+    rows = part.shape[1]
+    here = pl.ds(pl.multiple_of(s * rows, rows), rows)
+    for c in range(0, wide, CHUNK):
+        gate = dot(blocks[here], gu[:, c:c + CHUNK], 1, 0)
+        up = dot(blocks[here], gu[:, wide + c:wide + c + CHUNK], 1, 0)
+        act[here, c:c + CHUNK] = (gate * jax.nn.sigmoid(gate) * up).astype(BF16)
+    part[s] = dot(act[here], down[...], 1, 0)
+
+
+def backward_block(s, blocks, part, inputs, outputs):
+    gu, down, normed = inputs[:3]
+    d_gu = outputs[0]
+    wide = down.shape[0]
+    rows = part.shape[1]
+    here = pl.ds(pl.multiple_of(s * rows, rows), rows)
+    for c in range(0, wide, CHUNK):
+        gate = dot(normed[here], gu[:, c:c + CHUNK], 1, 0)
+        up = dot(normed[here], gu[:, wide + c:wide + c + CHUNK], 1, 0)
+        d_act = dot(blocks[here], down[c:c + CHUNK], 1, 1)
+        sig = jax.nn.sigmoid(gate)
+        d_gu[here, c:c + CHUNK] = (d_act * up * sig * (1.0 + gate * (1.0 - sig))).astype(BF16)
+        d_gu[here, wide + c:wide + c + CHUNK] = (d_act * (gate * sig)).astype(BF16)
+    part[s] = dot(d_gu[here], gu[...], 1, 1)
+
+
+def exchange(compute, collective_id, own, inputs, extra_shape, products, reduced=False):
+    rows, width = own.shape
+    vmem = pl.BlockSpec(memory_space=pltpu.VMEM)
+    n_inputs = 1 + len(inputs)
+    n_outputs = 4 if reduced else 3
+    shapes = [jax.ShapeDtypeStruct((8 * rows, width), BF16), jax.ShapeDtypeStruct((rows, width), F32), jax.ShapeDtypeStruct(extra_shape, BF16)]
+    scratch = []
+    if reduced:
+        shapes.append(jax.ShapeDtypeStruct((8, width + 128), F32))
+        scratch = [pltpu.VMEM((3, 8, width + 128), F32), pltpu.VMEM((3, 8, width + 128), F32), pltpu.SemaphoreType.DMA((3,)),
+                   pltpu.SemaphoreType.DMA((3,))]
+    return pl.pallas_call(
+        functools.partial(exchange_kernel, compute, n_inputs, n_outputs, reduced),
+        in_specs=[vmem] * n_inputs,
+        out_specs=[vmem] * n_outputs,
+        out_shape=shapes,
+        scratch_shapes=[pltpu.VMEM((8, rows, width), F32), pltpu.VMEM((4, rows, width), F32),
+                        pltpu.VMEM((rows // 2, width), F32), pltpu.VMEM((rows // 2, width), F32),
+                        pltpu.VMEM((rows, width), F32), pltpu.VMEM((rows, width), F32),
+                        pltpu.SemaphoreType.DMA((8,)), pltpu.SemaphoreType.DMA((8,)), pltpu.SemaphoreType.DMA((4,)),
+                        pltpu.SemaphoreType.DMA((4,)), pltpu.SemaphoreType.DMA((6,)), pltpu.SemaphoreType.DMA((6,))] + scratch,
+        compiler_params=pltpu.CompilerParams(collective_id=collective_id, has_side_effects=True, vmem_limit_bytes=VMEM),
+        cost_estimate=pl.CostEstimate(flops=products * 2 * 8 * rows * width * extra_shape[1] // 2, bytes_accessed=40_000_000, transcendentals=0),
+    )(own, *inputs)
+
+
 def lane_lse(m, l):
     top = jnp.max(m, axis=1, keepdims=True)
     return top, jnp.sum(l * jnp.exp(m - top), axis=1, keepdims=True)
@@ -261,13 +466,7 @@
         inv_rms = lax.rsqrt(jnp.mean(h1 * h1, axis=-1, keepdims=True) + NORM_EPS)
         normed = (h1 * inv_rms * gain).astype(BF16)
 
-        normed_all = gather(normed)
-        pre = dot(normed_all, gu, 1, 0)
-        gate_pre, up_pre = pre[:, :wide], pre[:, wide:]
-        gate_sig = jax.nn.sigmoid(gate_pre)
-        gate_act = gate_pre * gate_sig
-        act = (gate_act * up_pre).astype(BF16)
-        mlp_out = lax.psum_scatter(dot(act, down, 1, 0), AXIS_NAME, scatter_dimension=0, tiled=True)
+        normed_all, mlp_out, act = exchange(forward_block, 1, normed, (gu, down), (n * rows, wide), 3)
         draft_out = (h1 + mlp_out).astype(BF16)
 
         draft_pair = jnp.concatenate([draft_out, swap(draft_out)], axis=0)
@@ -300,14 +499,10 @@
         local_loss = reg_total - CLS_WEIGHT * jnp.sum(cross * valid)
 
         d_out = (jnp.clip(error, -1.0, 1.0) * (inv_count / width) + dy_own) * valid[:rows]
-        d_out_all = gather(d_out.astype(BF16))
-        d_act = dot(d_out_all, down, 1, 1)
-        d_gate = (d_act * up_pre * gate_sig * (1.0 + gate_pre * (1.0 - gate_sig))).astype(BF16)
-        d_up = (d_act * gate_act).astype(BF16)
-        d_gu = jnp.concatenate([d_gate, d_up], axis=1)
-        d_normed = lax.psum_scatter(dot(d_gu, gu, 1, 1), AXIS_NAME, scatter_dimension=0, tiled=True)
+        d_out_all, d_normed, d_gu, sums = exchange(backward_block, 2, d_out.astype(BF16),
+                                                   (gu, down, normed_all, h1 * inv_rms, jnp.full((8, 128), local_loss, F32)),
+                                                   (n * rows, 2 * wide), 5, True)
         grad_gu = dot(normed_all, d_gu, 0, 0).reshape(n, shard, 2 * wide)
-        d_normed, grad_gu = lax.optimization_barrier((d_normed, grad_gu))
         grad_gu = spread(grad_gu)
         grad_gate = jnp.concatenate([grad_gu[j][:, :ends[j] - starts[j]] for j in range(n)], axis=1)
         grad_up = jnp.concatenate([grad_gu[j][:, wide:wide + ends[j] - starts[j]] for j in range(n)], axis=1)
@@ -319,9 +514,8 @@
         gained = d_normed * gain
         d_hidden1 = d_out + inv_rms * gained - h1 * (inv_rms * inv_rms * inv_rms) * jnp.mean(gained * h1, axis=-1, keepdims=True)
         d_h1 = d_hidden1.astype(BF16)
-        sums = lax.psum(jnp.concatenate([jnp.sum(d_normed * h1 * inv_rms, axis=0), jnp.full((128,), local_loss, F32)]), AXIS_NAME)
-        total_loss = sums[width] * inv_count
-        grad_gain = lax.dynamic_slice(sums, (me * shard,), (shard,))
+        total_loss = sums[0, width] * inv_count
+        grad_gain = lax.dynamic_slice(sums[0], (me * shard,), (shard,))
         d_h1_all = gather(d_h1)
         d_mixed = dot(d_h1, o_full, 1, 1).astype(BF16)
         d_q, d_k, d_v = attn_vjp(d_mixed.reshape(mixed.shape))

time: 1180 us -> 1040 us (0.88)
  the two profiles are of different devices: /device:TPU:0 before, /device:TPU:1 now
where the time goes in v2:
time: 1040 us; the launch traced here: 1030 us
  Pallas kernels  608 us (58%)
  waiting for transfers between devices  189 us (18%)
  local copies, waits for them, and re-layouts  72.8 us (7%)
  matrix products  71.3 us (7%)
  other arithmetic  50.8 us (5%)
  starting transfers between devices  20.5 us (2%)
  between operations  18.9 us (2%)
    pallas_call x2, Pallas kernels, logits_pass(): pl.pallas_call(logits_kernel, grid_spec=pltpu.PrefetchScalarGridSpec(num_...  272 us
    ppermute x1, waiting for transfers between devices, local_step(): lax.ppermute(grad_down[wide - edge:], AXIS_NAME, [(j, j + 1) for j in ran...  186 us
    pallas_call x2, Pallas kernels, exchange(): pl.pallas_call(functools.partial(exchange_kernel, compute, n_inputs, n_ou...  181 us
    pallas_call x1, Pallas kernels, grad_pass(): pl.pallas_call(functools.partial(grad_kernel, steps), grid_spec=pltpu.Pre...  155 us
    dot_general x11, matrix products, dot(): lax.dot_general(a, b, (((ca,), (cb,)), ((), ())), preferred_element_type=...  65.2 us
    unnamed x196, local copies, waits for them, and re-layouts  29.7 us
  transfers between devices with their start and end apart: 14, of which 2 were waited for; matrix products, arithmetic and copies ran while one was open for 12% of the time, Pallas kernels for 28%

profile of v2, /device:TPU:1, one launch (start us, length us, event | category | flops | bytes accessed | tf_op | source)
XLA Modules:
  0.0 1031.6 jit_solution(4397033282903152223)
XLA Ops:
  12.1 2.4 collective-permute-start.1
  18.0 2.1 copy-done.5
  20.6 1.8 copy-done.23
  22.4 5.3 pad_maximum_fusion
  27.8 3.9 all-to-all-start
  34.0 6.2 gather_fusion
  40.9 6.4 fusion.13.refs_2_
  48.6 136.2 %vocab_logits.2 = (f32[384,76032]{1,0:T(8,128)}, f32[384,128]{1,0:T(8,128)}, f32[384,128]{1,0:T(8,128)}) custom-call(s32[2]{0:T(128)} %pad_add_fusion.info_ref, bf16[384,1536]{1,0:T(8,128)(2,1)} %pad_maximum_fusion.2.x_ref, bf16[151936,1536]{1,0:T(8,128)(2,1)} %hc_ref.5, bf16[151936,1536]{1,0:T(8,128)(2,1)} %hc_ref.5, bf16[151936,1536]{1,0:T(8,128)(2,1)} %hc_ref.5), custom_call_target="tpu_custom_call" | custom-call | flops 89690996736 | bytes 350355456 | tf_op jit(solution)/shard_map/vocab_logits/pallas_call | solution.py:96
  184.9 3.5 fusion.26
  188.4 1.5 all-gather.8.cloned.1.call-done
  189.9 1.5 convert_reduce_fusion.1
  191.5 3.4 fusion.35
  195.7 4.2 fusion.3
  205.2 1.5 reshape.241
  206.7 3.7 multiply_reduce_fusion.1
  211.0 1.5 multiply_convert_fusion
  212.5 81.7 %shard_map.221 = (bf16[1536,1536]{1,0:T(8,128)(2,1)}, f32[192,1536]{1,0:T(8,128)}, bf16[1536,1152]{1,0:T(8,128)(2,1)}) custom-call(bf16[192,1536]{1,0:T(8,128)(2,1)} %get-tuple-element.107.refs_0_, bf16[1536,2304]{1,0:T(8,128)(2,1)} %bitcast.30.refs_1_, bf16[1152,1536]{1,0:T(8,128)(2,1)} %fusion.13.refs_2_), custom_call_target="tpu_custom_call" | custom-call | flops 8153726976 | bytes 40000000 | tf_op jit(solution)/shard_map/pallas_call | solution.py:365
  294.3 2.4 fusion.57
  296.7 1.6 collective-permute-start.2
  298.3 1.6 concatenate.78
  299.9 1.6 concatenate.77
  302.1 1.6 maximum_bitcast_fusion
  305.3 1.6 reshape.244
  306.9 1.5 reshape.243
  308.4 2.2 pad_maximum_fusion.3.x_ref
  310.6 135.5 %vocab_logits.3 = (f32[384,76032]{1,0:T(8,128)}, f32[384,128]{1,0:T(8,128)}, f32[384,128]{1,0:T(8,128)}) custom-call(s32[2]{0:T(128)} %pad_add_fusion.info_ref, bf16[384,1536]{1,0:T(8,128)(2,1)} %pad_maximum_fusion.3.x_ref, bf16[151936,1536]{1,0:T(8,128)(2,1)} %hc_ref.5, bf16[151936,1536]{1,0:T(8,128)(2,1)} %hc_ref.5, bf16[151936,1536]{1,0:T(8,128)(2,1)} %hc_ref.5), custom_call_target="tpu_custom_call" | custom-call | flops 89690996736 | bytes 350355456 | tf_op jit(solution)/shard_map/vocab_logits/pallas_call | solution.py:96
  447.2 1.3 multiply_reduce_fusion.3
  449.3 1.9 copy.92
  451.2 3.4 all-to-all-start.1
  457.1 155.4 %vocab_grad.1 = (f32[384,1536]{1,0:T(8,128)}, f32[384,128]{1,0:T(8,128)}) custom-call(s32[2]{0:T(128)} %pad_add_fusion.info_ref, f32[384,76032]{1,0:T(8,128)} %get-tuple-element.37.zt_ref, f32[384,76032]{1,0:T(8,128)} %get-tuple-element.38.zq_ref, bf16[151936,1536]{1,0:T(8,128)(2,1)} %hc_ref.5, bf16[151936,1536]{1,0:T(8,128)(2,1)} %hc_ref.5, ...), custom_call_target="tpu_custom_call" | custom-call | flops 89690996736 | bytes 467140608 | tf_op jit(solution)/shard_map/vocab_grad/pallas_call | solution.py:161
  612.6 1.4 slice.301
  615.4 1.4 multiply_divide_fusion
  616.7 1.6 multiply_reduce_fusion.2
  619.1 2.5 fusion.99
  622.2 99.5 %shard_map.222 = (bf16[1536,1536]{1,0:T(8,128)(2,1)}, f32[192,1536]{1,0:T(8,128)}, bf16[1536,2304]{1,0:T(8,128)(2,1)}, f32[8,1664]{1,0:T(8,128)}) custom-call(bf16[192,1536]{1,0:T(8,128)(2,1)} %get-tuple-element.105.refs_0_, bf16[1536,2304]{1,0:T(8,128)(2,1)} %bitcast.30.refs_1_, bf16[1152,1536]{1,0:T(8,128)(2,1)} %fusion.13.refs_2_, ...), custom_call_target="tpu_custom_call" | custom-call | flops 27179089920 | bytes 40000000 | tf_op jit(solution)/shard_map/pallas_call | solution.py:365
  721.8 1.6 multiply_reduce_fusion
  723.4 1.4 fusion.98
  724.7 4.2 fusion.29
  729.1 1.5 reshape_reshape.3
  730.6 1.5 fusion.64
  732.2 2.0 fusion.55
  736.7 1.5 fusion.44
  739.0 1.4 copy-done.38
  740.3 5.8 fusion.32
  746.7 17.4 %fusion.104 = f32[1536,2304]{1,0:T(8,128)} fusion(bf16[1536,1536]{1,0:T(8,128)(2,1)} %get-tuple-element.45.refs_3_, bf16[1536,2304]{1,0:T(8,128)(2,1)} %get-tuple-element.50), kind=kOutput, calls=%fused_computation.214 | convolution fusion | flops 10871635968 | bytes 25952256 | tf_op jit(solution)/shard_map/dot_general | solution.py:26
  764.1 4.9 all-to-all-start.2
  769.6 8.8 fusion.105
  778.4 2.9 copy-done.12
  781.3 3.8 collective-permute-start.5
  786.0 1.2 slice.302
  788.5 185.6 %collective-permute-done.5 = f32[96,1536]{1,0:T(8,128)S(1)} collective-permute-done((f32[96,1536]{1,0:T(8,128)S(1)}, f32[96,1536]{1,0:T(8,128)S(1)}, u32[]{:S(2)}, u32[]{:S(2)}) %collective-permute-start.5) | collective-permute-done | bytes 589856 | tf_op jit(solution)/shard_map/ppermute | solution.py:511
  974.0 6.7 fusion
  980.8 2.2 convert_reduce_fusion
  983.0 4.9 fusion.66
  987.9 4.7 fusion.58
  992.6 4.5 fusion.68
  999.8 9.8 slice_bitcast_fusion
  1009.6 1.7 slice_dynamic-update-slice_fusion.5
  1011.7 1.4 copy-done.15
  1013.2 1.3 copy-done.18
  1015.2 1.4 copy-done.13
  1016.8 1.3 copy-done.17
  1018.3 2.9 copy-done.66
  1021.2 2.3 copy-done.67
  (285 shorter events, 37.4 us)
Async XLA Ops:
  7.2 2.3 copy-start
  7.2 2.4 copy-start.68
  7.2 2.4 copy-start.69
  7.2 2.5 copy-start.46
  7.2 177.6 %all-gather.6.cloned.1.call-start = ((), (), s32[]{:S(2)}) async-start(), calls=%async_computation.3 | async-start | bytes 10616832 | tf_op jit(solution)/shard_map/all_gather | solution.py:392
  8.0 181.9 %all-gather.8.cloned.1.call-start = ((), (), s32[]{:S(2)}) async-start(), calls=%async_computation.4 | async-start | bytes 12828672 | tf_op jit(solution)/shard_map/all_gather | solution.py:392
  10.9 6.9 copy-start.6
  10.9 36.4 %collective-permute-start = (bf16[192,1536]{1,0:T(8,128)(2,1)S(1)}, bf16[192,1536]{1,0:T(8,128)(2,1)S(1)}, u32[]{:S(2)}, u32[]{:S(2)}) collective-permute-start(bf16[192,1536]{1,0:T(8,128)(2,1)S(1)} %bitcast.190), channel_id=1, source_target_pairs={{0,1},{1,0},{2,3},{3,2},{4,5},{5,4},{6,7},{7,6}} | collective-permute-start | bytes 1769480 | tf_op jit(solution)/shard_map/ppermute | solution.py:395
  12.1 28.8 %collective-permute-start.1 = (bf16[128,1536]{1,0:T(8,128)(2,1)S(1)}, bf16[128,1536]{1,0:T(8,128)(2,1)S(1)}, u32[]{:S(2)}, u32[]{:S(2)}) collective-permute-start(bf16[128,1536]{1,0:T(8,128)(2,1)S(1)} %slice.292), channel_id=1, source_target_pairs={{1,0},{2,1},{3,2},{5,4},{6,5},{7,6}} | collective-permute-start | bytes 1179656 | tf_op jit(solution)/shard_map/ppermute | solution.py:448
  17.8 2.3 copy-start.5
  27.8 3.9 copy-start.83
  27.8 184.7 %all-to-all-start = ((bf16[8,192,2304]{2,1,0:T(8,128)(2,1)}), bf16[8,192,2304]{2,1,0:T(8,128)(2,1)}, u32[]{:S(2)}, u32[]{:S(2)}) async-start(bf16[8,192,2304]{2,1,0:T(8,128)(2,1)} %pad_maximum_fusion), calls=%async_computation | async-start | bytes 14155776 | tf_op jit(solution)/shard_map/all_to_all | solution.py:398
  40.8 6.7 copy-start.9
  48.6 136.3 %copy-start.28 = (bf16[3,64,1536]{2,1,0:T(8,128)(2,1)S(1)}, bf16[3,64,1536]{2,1,0:T(8,128)(2,1)}, u32[]{:S(2)}) copy-start(bf16[3,64,1536]{2,1,0:T(8,128)(2,1)} %param.14) | copy-start | bytes 1769476
  184.9 6.6 copy-start.30
  191.4 19.6 %copy-start.62 = (f32[1536]{0:T(1024)}, f32[1536]{0:T(1024)S(1)}, u32[]{:S(2)}) copy-start(f32[1536]{0:T(1024)S(1)} %get-tuple-element.97) | copy-start | bytes 18436
  204.4 2.3 copy-start.31
  204.4 2.3 copy-start.48
  210.4 83.8 %copy-start.3 = (f32[192,1536]{1,0:T(8,128)}, f32[192,1536]{1,0:T(8,128)S(1)}, u32[]{:S(2)}) copy-start(f32[192,1536]{1,0:T(8,128)S(1)} %get-tuple-element.156) | copy-start | bytes 3538948
  212.5 81.8 %copy-start.10 = (bf16[3,64,1536]{2,1,0:T(8,128)(2,1)S(1)}, bf16[3,64,1536]{2,1,0:T(8,128)(2,1)}, u32[]{:S(2)}) copy-start(bf16[3,64,1536]{2,1,0:T(8,128)(2,1)} %copy-done.9) | copy-start | bytes 1769476
  212.5 81.8 %copy-start.81 = (f32[192,1]{0,1:T(1,128)S(1)}, f32[192,1]{0,1:T(1,128)}, u32[]{:S(2)}) copy-start(f32[192,1]{0,1:T(1,128)} %compare_convert_fusion) | copy-start | bytes 2308
  296.7 11.8 %copy-start.19 = (bf16[192,1536]{1,0:T(8,128)(2,1)}, bf16[192,1536]{1,0:T(8,128)(2,1)S(1)}, u32[]{:S(2)}) copy-start(bf16[192,1536]{1,0:T(8,128)(2,1)S(1)} %get-tuple-element.104) | copy-start | bytes 1769476
  296.7 11.8 %collective-permute-start.2 = (bf16[192,1536]{1,0:T(8,128)(2,1)S(1)}, bf16[192,1536]{1,0:T(8,128)(2,1)}, u32[]{:S(2)}, u32[]{:S(2)}) collective-permute-start(bf16[192,1536]{1,0:T(8,128)(2,1)S(1)} %get-tuple-element.104), channel_id=1, source_target_pairs={{0,1},{1,0},{2,3},{3,2},{4,5},{5,4},{6,7},{7,6}} | collective-permute-start | bytes 1769480 | tf_op jit(solution)/shard_map/ppermute | solution.py:395
  299.9 3.9 copy-start.45
  299.9 4.6 copy-start.61
  303.8 3.2 copy-start.49
  303.9 4.5 copy-start.70
  304.7 3.7 copy-start.73
  310.6 137.9 %copy-start.79 = (f32[384,1]{0,1:T(1,128)S(1)}, f32[384,1]{0,1:T(1,128)}, u32[]{:S(2)}) copy-start(f32[384,1]{0,1:T(1,128)} %reduce_max.31) | copy-start | bytes 4612
  310.6 137.9 %copy-start.80 = (f32[384,1]{0,1:T(1,128)S(1)}, f32[384,1]{0,1:T(1,128)}, u32[]{:S(2)}) copy-start(f32[384,1]{0,1:T(1,128)} %broadcast_in_dim.75) | copy-start | bytes 4612
  310.6 138.2 %copy-start.21 = (bf16[8,192,384]{2,0,1:T(8,128)(2,1)S(1)}, bf16[8,192,384]{2,0,1:T(8,128)(2,1)}, u32[]{:S(2)}) copy-start(bf16[8,192,384]{2,0,1:T(8,128)(2,1)} %maximum_bitcast_fusion) | copy-start | bytes 3538948
  310.6 138.2 %copy-start.24 = (bf16[192,8,192]{2,1,0:T(8,128)(2,1)S(1)}, bf16[192,8,192]{2,1,0:T(8,128)(2,1)}, u32[]{:S(2)}) copy-start(bf16[192,8,192]{2,1,0:T(8,128)(2,1)} %reshape.244) | copy-start | bytes 1769476
  310.6 138.2 %copy-start.25 = (bf16[192,8,192]{2,1,0:T(8,128)(2,1)S(1)}, bf16[192,8,192]{2,1,0:T(8,128)(2,1)}, u32[]{:S(2)}) copy-start(bf16[192,8,192]{2,1,0:T(8,128)(2,1)} %reshape.243) | copy-start | bytes 1769476
  448.5 6.1 collective-permute-start.3
  451.2 3.5 copy-start.71
  451.2 3.5 copy-start.74
  451.2 5.2 copy-start.77
  451.2 161.4 %all-to-all-start.1 = ((bf16[8,192,768]{2,1,0:T(8,128)(2,1)}), bf16[8,192,768]{2,1,0:T(8,128)(2,1)}, u32[]{:S(2)}, u32[]{:S(2)}) async-start(bf16[8,192,768]{2,1,0:T(8,128)(2,1)} %copy.92), calls=%async_computation.1 | async-start | bytes 4718592 | tf_op jit(solution)/shard_map/all_to_all | solution.py:398
  454.5 526.2 %all-gather.10.cloned.1.call-start = ((), (), s32[]{:S(2)}) async-start(), calls=%async_computation.5 | async-start | bytes 5308416 | tf_op jit(solution)/shard_map/all_gather | solution.py:392
  612.6 6.4 copy-start.11
  612.6 6.5 copy-start.20
  614.0 5.0 collective-permute-start.4
  622.2 99.6 %copy-start.4 = (f32[192,1536]{1,0:T(8,128)S(1)}, f32[192,1536]{1,0:T(8,128)}, u32[]{:S(2)}) copy-start(f32[192,1536]{1,0:T(8,128)} %copy-done.3) | copy-start | bytes 3538948
  622.2 99.6 %copy-start.63 = (f32[1536]{0:T(1024)S(1)}, f32[1536]{0:T(1024)}, u32[]{:S(2)}) copy-start(f32[1536]{0:T(1024)} %copy-done.62) | copy-start | bytes 18436
  724.7 4.3 copy-start.37
  724.7 5.9 copy-start.32
  729.0 3.1 copy-start.8
  729.0 3.1 copy-start.55
  729.0 3.1 copy-start.58
  729.0 3.1 copy-start.65
  729.0 3.1 copy-start.72
  732.1 2.0 copy-start.34
  732.1 2.0 copy-start.36
  732.1 2.0 copy-start.60
  739.0 7.2 copy-start.29
  746.2 236.8 %all-gather.14.cloned.1.call-start = ((), (), s32[]{:S(2)}) async-start(), calls=%async_computation.7 | async-start | bytes 5308416 | tf_op jit(solution)/shard_map/all_gather | solution.py:392
  764.1 235.6 %all-to-all-start.2 = ((f32[8,192,2304]{2,1,0:T(8,128)}), f32[8,192,2304]{2,1,0:T(8,128)}, u32[]{:S(2)}, u32[]{:S(2)}) async-start(f32[8,192,2304]{2,1,0:T(8,128)} %bitcast.184), calls=%async_computation.2 | async-start | bytes 28311552 | tf_op jit(solution)/shard_map/all_to_all | solution.py:398
  769.0 223.6 %all-gather.12.cloned.1.call-start = ((), (), s32[]{:S(2)}) async-start(), calls=%async_computation.6 | async-start | bytes 7077888 | tf_op jit(solution)/shard_map/all_gather | solution.py:392
  778.4 2.9 copy-start.12
  781.3 192.7 %collective-permute-start.5 = (f32[96,1536]{1,0:T(8,128)S(1)}, f32[96,1536]{1,0:T(8,128)S(1)}, u32[]{:S(2)}, u32[]{:S(2)}) collective-permute-start(f32[96,1536]{1,0:T(8,128)S(1)} %slice.385), channel_id=1, source_target_pairs={{0,1},{1,2},{2,3},{4,5},{5,6},{6,7}} | collective-permute-start | bytes 1769480 | tf_op jit(solution)/shard_map/ppermute | solution.py:511
  983.0 4.9 copy-start.2
  1016.7 6.7 copy-start.1
  1018.3 2.9 copy-start.66
  1018.3 5.2 copy-start.67
  (34 other events, 44.5 us)
Sparse Core Ops, SparseCore 0:
  9.8 103.3 all-gather.5
  115.6 74.2 all-gather.7
  746.3 40.0 all-gather.9
  788.6 110.1 all-gather.13
  901.0 77.3 all-gather.11
